TPU v7x, 256 devices: a whole 4x4x8 slice. The times are simulated.
256 devices in a mesh: rep: 1, r: 4 (over x), s: 64 (over y, z, core).
Axes of the slice: x: 4, y: 4, z: 8, core: 2. Of those that a mesh axis runs over, the one named last changes fastest.
Arguments:
- x: bfloat16 [256, 2048, 640], P(('rep', 'r', 's'))
- dy: bfloat16 [256, 2048, 640], P(('rep', 'r', 's'))
- w_gate: bfloat16 [2, 640, 2560], P(None, 's')
- w_up: bfloat16 [2, 640, 2560], P(None, 's')
- w_down: bfloat16 [2, 2560, 640], P(None, 's')
Outputs:
- output 1: bfloat16 [256, 2048, 640], P(('rep', 'r', 's'))
- output 2: bfloat16 [2, 640, 2560], P('rep', 's')
- output 3: bfloat16 [2, 640, 2560], P('rep', 's')
- output 4: bfloat16 [2, 2560, 640], P('rep', 's')
All inputs are finite; a program needn't handle non-finite values.
Results may differ from a plain program's by a relative error of at most 0.018.
Values are sent between devices in bfloat16 or wider.
A program may use at most 768 MiB of HBM per device.

v0:
```python
import jax
import jax.numpy as jnp
from jax import lax
from jax.sharding import PartitionSpec as P

NAMES = ("w_gate", "w_up", "w_down")


def matmul(a, w):
    return jnp.dot(a, w, preferred_element_type=jnp.float32).astype(jnp.bfloat16)


def normed(h):
    wide = h.astype(jnp.float32)
    scale = lax.rsqrt(jnp.mean(wide**2, -1, keepdims=True) + 1e-6)
    return (wide * scale).astype(jnp.bfloat16)


def layer(h, w):
    a = normed(h)
    gate = jnp.dot(a, w["w_gate"], preferred_element_type=jnp.float32)
    up = jnp.dot(a, w["w_up"], preferred_element_type=jnp.float32)
    return h + matmul((jax.nn.silu(gate) * up).astype(jnp.bfloat16), w["w_down"])


def solution(mesh):
    def fetched(weights, number):
        return {name: lax.all_gather(w[number], "s", axis=0, tiled=True) for name, w in zip(NAMES, weights, strict=True)}

    def summed(term):
        return lax.psum(lax.psum_scatter(term, "s", scatter_dimension=0, tiled=True), "r")

    def step(x, dy, *weights):
        layers = weights[0].shape[0]
        h, inputs = x[0], []
        for number in range(layers):
            inputs.append(h)
            h = layer(h, fetched(weights, number))
        by_h, mine = dy[0], [None] * layers
        for number in reversed(range(layers)):
            _, back = jax.vjp(lambda w, h: layer(h, w), fetched(weights, number), inputs[number])
            by_w, by_h = back(by_h)
            mine[number] = [summed(by_w[name]) for name in NAMES]
        return (by_h[None], *(jnp.stack([mine[number][i] for number in range(layers)]) for i in range(3)))

    states, cut = P(("rep", "r", "s"), None, None), P(None, "s", None)
    return jax.shard_map(
        step,
        mesh=mesh,
        in_specs=(states, states) + (cut,) * 3,
        out_specs=(states,) + (P("rep", "s", None),) * 3,
        check_vma=False,
    )
```

profile of v0, /device:TPU:1, one launch (start us, length us, event | category | flops | bytes accessed | tf_op | source)
XLA Modules:
  0.0 1196.2 jit_solution(14025036288455952878)
XLA Ops:
  7.2 1.8 fusion.95
  9.1 1.8 fusion.94
  11.0 1.5 fusion.93
  13.1 0.5 all-gather.23.cloned.1.call-update
  13.7 0.5 all-gather.19.cloned.1.call-update
  14.3 3.0 copy.24
  17.3 0.6 fusion.15
  17.9 0.9 copy-done.5
  18.8 4.5 copy.23
  23.3 73.0 %all-gather.13.cloned.1.call-done = bf16[1,640,2560]{2,0,1:T(2,128)(2,1)} async-done(((bf16[1,10,2560]{2,0,1:T(2,128)(2,1)}), bf16[1,640,2560]{2,0,1:T(2,128)(2,1)}) %all-gather.13.cloned.1.call-update) | async-done | bytes 3276816 | tf_op jit(solution)/shard_map/all_gather | solution.py:28
  96.3 14.3 %fusion.36 = f32[2048,2560]{1,0:T(8,128)} fusion(bf16[1,2048,640]{1,2,0:T(8,128)(2,1)S(1)} %copy.24, f32[2048]{0:T(1024)S(1)} %fusion.86, bf16[1,640,2560]{2,0,1:T(2,128)(2,1)} %all-gather.13.cloned.1.call-done), kind=kOutput, calls=%fused_computation.61 | convolution fusion | flops 6714818560 | bytes 26877952 | tf_op jit(solution)/shard_map/dot_general | solution.py:21
  110.6 66.6 %all-gather.15.cloned.1.call-done = bf16[1,640,2560]{2,0,1:T(2,128)(2,1)} async-done(((bf16[1,10,2560]{2,0,1:T(2,128)(2,1)}), bf16[1,640,2560]{2,0,1:T(2,128)(2,1)}) %all-gather.15.cloned.1.call-update) | async-done | bytes 3276816 | tf_op jit(solution)/shard_map/all_gather | solution.py:28
  177.2 22.8 %multiply_convert_fusion.1 = (bf16[2048,2560]{1,0:T(8,128)(2,1)}, f32[2048,2560]{1,0:T(8,128)}) fusion(f32[2048,2560]{1,0:T(8,128)} %fusion.36, bf16[1,640,2560]{2,0,1:T(2,128)(2,1)} %all-gather.15.cloned.1.call-done, bf16[1,2048,640]{1,2,0:T(8,128)(2,1)S(1)} %copy.24, f32[2048]{0:T(1024)S(1)} %fusion.86), kind=kOutput, calls=%fused_computation.13 | convolution fusion | flops 6746275840 | bytes 58335232 | tf_op jit(solution)/shard_map/dot_general | solution.py:22
  200.0 54.9 %all-gather.17.cloned.1.call-done = bf16[1,2560,640]{2,1,0:T(8,128)(2,1)} async-done(((bf16[1,40,640]{2,1,0:T(8,128)(2,1)}), bf16[1,2560,640]{2,1,0:T(8,128)(2,1)}) %all-gather.17.cloned.1.call-update) | async-done | bytes 3276816 | tf_op jit(solution)/shard_map/all_gather | solution.py:28
  254.9 12.0 %fusion.18 = (f32[2048]{0:T(1024)S(1)}, bf16[2048,640]{0,1:T(8,128)(2,1)}) fusion(bf16[2048,2560]{1,0:T(8,128)(2,1)} %get-tuple-element.32, bf16[1,2560,640]{2,1,0:T(8,128)(2,1)} %all-gather.17.cloned.1.call-done, bf16[1,2048,640]{1,2,0:T(8,128)(2,1)S(1)} %copy.24), kind=kOutput, calls=%fused_computation.40 | convolution fusion | flops 6717437952 | bytes 19013632 | tf_op jit(solution)/shard_map/dot_general | solution.py:10
  266.9 0.6 copy-done.9
  267.5 65.5 %all-gather.21.cloned.1.call-done = bf16[1,2560,640]{2,1,0:T(8,128)(2,1)} async-done(((bf16[1,40,640]{2,1,0:T(8,128)(2,1)}), bf16[1,2560,640]{2,1,0:T(8,128)(2,1)}) %all-gather.21.cloned.1.call-update) | async-done | bytes 3276816 | tf_op jit(solution)/shard_map/all_gather | solution.py:28
  333.0 13.5 %convolution_convert_fusion.1 = bf16[2048,2560]{1,0:T(8,128)(2,1)} fusion(bf16[1,2560,640]{2,1,0:T(8,128)(2,1)} %all-gather.21.cloned.1.call-done, bf16[1,2048,640]{2,1,0:T(8,128)(2,1)} %param.6), kind=kOutput, calls=%fused_computation.21 | convolution fusion | flops 6716129280 | bytes 16384000 | tf_op jit(solution)/shard_map/transpose(jvp())/dot_general | solution.py:10
  346.4 67.8 %all-gather.23.cloned.1.call-done = bf16[1,640,2560]{2,0,1:T(2,128)(2,1)} async-done(((bf16[1,10,2560]{2,0,1:T(2,128)(2,1)}), bf16[1,640,2560]{2,0,1:T(2,128)(2,1)}) %all-gather.23.cloned.1.call-update) | async-done | bytes 3276816 | tf_op jit(solution)/shard_map/all_gather | solution.py:28
  414.2 14.3 %fusion.24 = f32[2048,2560]{1,0:T(8,128)} fusion(bf16[2048,640]{0,1:T(8,128)(2,1)S(1)} %copy-done.4, f32[2048]{0:T(1024)S(1)} %fusion.87, bf16[1,640,2560]{2,0,1:T(2,128)(2,1)} %all-gather.23.cloned.1.call-done), kind=kOutput, calls=%fused_computation.49 | convolution fusion | flops 6714818560 | bytes 26877952 | tf_op jit(solution)/shard_map/jvp()/dot_general | solution.py:22
  428.6 66.4 %all-gather.19.cloned.1.call-done = bf16[1,640,2560]{2,0,1:T(2,128)(2,1)} async-done(((bf16[1,10,2560]{2,0,1:T(2,128)(2,1)}), bf16[1,640,2560]{2,0,1:T(2,128)(2,1)}) %all-gather.19.cloned.1.call-update) | async-done | bytes 3276816 | tf_op jit(solution)/shard_map/all_gather | solution.py:28
  495.0 29.1 %fusion.1 = (bf16[2048,2560]{1,0:T(8,128)(2,1)}, f32[2048,2560]{1,0:T(8,128)}) fusion(f32[2048,2560]{1,0:T(8,128)} %fusion.24, bf16[2048,2560]{1,0:T(8,128)(2,1)} %convolution_convert_fusion.1, bf16[1,640,2560]{2,0,1:T(2,128)(2,1)} %all-gather.19.cloned.1.call-done, bf16[2048,640]{0,1:T(8,128)(2,1)S(1)} %copy-done.4, f32[2048]{0:T(1024)S(1)} %fusion.87), kind=kOutput, calls=%fused_computation.7 | convolution fusion | flops 6777733120 | bytes 68820992 | tf_op jit(solution)/shard_map/jvp()/dot_general | solution.py:21
  524.1 15.7 %fusion.23 = bf16[640,2560]{1,0:T(8,128)(2,1)} fusion(bf16[2048,2560]{1,0:T(8,128)(2,1)} %convolution_convert_fusion.1, bf16[2048,640]{0,1:T(8,128)(2,1)S(1)} %copy-done.4, f32[2048]{0:T(1024)S(1)} %fusion.87, f32[2048,2560]{1,0:T(8,128)} %get-tuple-element.37), kind=kOutput, calls=%fused_computation.45 | convolution fusion | flops 6747914240 | bytes 37363712 | tf_op jit(solution)/shard_map/transpose(jvp())/dot_general | solution.py:22
  539.7 11.0 convolution_convert_fusion.3
  550.7 8.2 fusion.48
  559.0 22.0 %fusion.20 = (f32[2048]{0:T(1024)S(1)}, bf16[2048,640]{0,1:T(8,128)(2,1)}) fusion(bf16[2048,640]{0,1:T(8,128)(2,1)} %get-tuple-element.35, bf16[2048,640]{0,1:T(8,128)(2,1)} %fusion.48, bf16[1,640,2560]{2,0,1:T(2,128)(2,1)} %all-gather.23.cloned.1.call-done, bf16[2048,2560]{1,0:T(8,128)(2,1)} %convolution_convert_fusion.1, f32[2048,2560]{1,0:T(8,128)} %get-tuple-element.37), kind=kOutput, calls=%fused_computation.42 | convolution fusion | flops 6750205952 | bytes 42606592 | tf_op jit(solution)/shard_map/transpose(jvp())/dot_general | solution.py:22
  581.0 4.5 fusion.59
  585.5 25.6 %fusion.3 = (bf16[2048,2560]{1,0:T(8,128)(2,1)}, bf16[2048,2560]{1,0:T(8,128)(2,1)}) fusion(f32[2048,2560]{1,0:T(8,128)} %fusion.36, f32[2048,2560]{1,0:T(8,128)} %get-tuple-element.33, bf16[2048,640]{0,1:T(8,128)(2,1)S(1)} %fusion.59, bf16[1,2560,640]{2,1,0:T(8,128)(2,1)S(1)} %copy-done.12), kind=kOutput, calls=%fused_computation.9 | convolution fusion | flops 6779043840 | bytes 68812800 | tf_op jit(solution)/shard_map/transpose(jvp())/dot_general | solution.py:10
  611.1 15.5 %fusion.22 = bf16[640,2560]{1,0:T(8,128)(2,1)} fusion(bf16[2048,2560]{1,0:T(8,128)(2,1)} %get-tuple-element.41, bf16[1,2048,640]{1,2,0:T(8,128)(2,1)S(1)} %copy-done.1, f32[2048]{0:T(1024)S(1)} %copy-done.8, f32[2048,2560]{1,0:T(8,128)} %fusion.36), kind=kOutput, calls=%fused_computation.44 | convolution fusion | flops 6747914240 | bytes 37363712 | tf_op jit(solution)/shard_map/transpose(jvp())/dot_general | solution.py:22
  626.6 10.9 convolution_convert_fusion.4
  637.6 13.1 %convolution_convert_fusion.2 = bf16[2560,640]{1,0:T(8,128)(2,1)} fusion(bf16[2048,2560]{1,0:T(8,128)(2,1)} %get-tuple-element.32, bf16[2048,640]{0,1:T(8,128)(2,1)} %copy-done.2), kind=kOutput, calls=%fused_computation.46 | convolution fusion | flops 6712524800 | bytes 16384000 | tf_op jit(solution)/shard_map/transpose(jvp())/dot_general | solution.py:10
  650.8 0.6 dynamic-slice
  652.0 20.1 %fusion.21 = bf16[2560,640]{1,0:T(8,128)(2,1)} fusion(f32[2048,2560]{1,0:T(8,128)} %fusion.24, bf16[1,2048,640]{2,1,0:T(8,128)(2,1)} %param.6, f32[2048,2560]{1,0:T(8,128)} %get-tuple-element.37), kind=kOutput, calls=%fused_computation.43 | convolution fusion | flops 6743982080 | bytes 47841280 | tf_op jit(solution)/shard_map/transpose(jvp())/dot_general | solution.py:10
  672.2 12.8 %fusion.45 = bf16[2048,640]{0,1:T(8,128)(2,1)} fusion(bf16[2048,2560]{1,0:T(8,128)(2,1)} %get-tuple-element.40, bf16[1,640,2560]{2,0,1:T(2,128)(2,1)} %all-gather.13.cloned.1.call-done), kind=kOutput, calls=%fused_computation.68 | convolution fusion | flops 6710886400 | bytes 16384000 | tf_op jit(solution)/shard_map/transpose(jvp())/dot_general | solution.py:21
  685.0 19.9 %fusion.17 = (f32[2048]{0:T(1024)S(1)}, bf16[2048,640]{0,1:T(8,128)(2,1)}) fusion(bf16[1,2048,640]{1,2,0:T(8,128)(2,1)S(1)} %copy-done.1, bf16[2048,640]{0,1:T(8,128)(2,1)} %fusion.45, bf16[1,640,2560]{2,0,1:T(2,128)(2,1)} %all-gather.15.cloned.1.call-done, bf16[2048,2560]{1,0:T(8,128)(2,1)} %get-tuple-element.41, f32[2048,2560]{1,0:T(8,128)} %fusion.36), kind=kOutput, calls=%fused_computation.39 | convolution fusion | flops 6750205952 | bytes 42606592 | tf_op jit(solution)/shard_map/transpose(jvp())/dot_general | solution.py:22
  704.9 144.8 %all-reduce.11.cloned.1.call-done = (bf16[640,2560]{1,0:T(8,128)(2,1)}, bf16[640,2560]{1,0:T(8,128)(2,1)}, bf16[640,2560]{1,0:T(8,128)(2,1)}, bf16[640,2560]{1,0:T(8,128)(2,1)}) async-done(((bf16[640,2560]{1,0:T(8,128)(2,1)}, bf16[640,2560]{1,0:T(8,128)(2,1)}, bf16[640,2560]{1,0:T(8,128)(2,1)}, bf16[640,2560]{1,0:T(8,128)(2,1)}), (bf16[640,2560]{1,0:T(8,128)(2,1)}, bf16[640,2560]{1,0:T(8,128)(2,1)}, ...) | async-done | bytes 13107216
  849.6 1.7 dynamic-slice_bitcast_fusion
  851.3 1.7 dynamic-slice_bitcast_fusion.2
  853.0 135.2 %reduce-scatter.7.cloned.1.call-done = bf16[40,640]{1,0:T(8,128)(2,1)} async-done(((bf16[2560,640]{1,0:T(8,128)(2,1)}), bf16[40,640]{1,0:T(8,128)(2,1)}) %reduce-scatter.7.cloned.1.call-update) | async-done | bytes 51216
  988.2 143.0 %reduce-scatter.9.cloned.1.call-done = bf16[40,640]{1,0:T(8,128)(2,1)} async-done(((bf16[2560,640]{1,0:T(8,128)(2,1)}), bf16[40,640]{1,0:T(8,128)(2,1)}) %reduce-scatter.9.cloned.1.call-update) | async-done | bytes 51216
  1131.2 5.8 fusion.58
  1137.0 4.4 copy.25
  1141.4 42.6 %all-reduce.13.cloned.1.call-done = (bf16[1,10,2560]{2,1,0:T(8,128)(2,1)}, bf16[1,10,2560]{2,1,0:T(8,128)(2,1)}, bf16[1,10,2560]{2,1,0:T(8,128)(2,1)}, bf16[1,10...) async-done(((bf16[1,10,2560]{2,1,0:T(8,128)(2,1)}, bf16[1,10,2560]{2,1,0:T(8,128)(2,1)}, bf16[1,10,2560]{2,1,0:T(8,128)(2,1)}, ...) | async-done | bytes 307216 | tf_op jit(solution)/shard_map/psum | solution.py:31
  1184.0 1.0 pad_maximum_fusion.1
  1184.9 0.7 copy.27
  1185.7 1.0 pad_maximum_fusion
  1186.6 0.7 copy.26
  1187.4 1.5 pad_maximum_fusion.2
  (50 shorter events, 1.1 us)
Async XLA Ops:
  7.2 89.1 %all-gather.13.cloned.1.call-start = ((), (), s32[]{:S(2)}) async-start(), calls=%async_computation.2 | async-start | bytes 6656000 | tf_op jit(solution)/shard_map/all_gather | solution.py:28
  9.1 168.1 %all-gather.15.cloned.1.call-start = ((), (), s32[]{:S(2)}) async-start(), calls=%async_computation.3 | async-start | bytes 6656000 | tf_op jit(solution)/shard_map/all_gather | solution.py:28
  11.0 243.9 %all-gather.17.cloned.1.call-start = ((), (), s32[]{:S(2)}) async-start(), calls=%async_computation.4 | async-start | bytes 3328000 | tf_op jit(solution)/shard_map/all_gather | solution.py:28
  12.5 320.5 %all-gather.21.cloned.1.call-start = ((), (), s32[]{:S(2)}) async-start(), calls=%async_computation.6 | async-start | bytes 3328000 | tf_op jit(solution)/shard_map/all_gather | solution.py:28
  13.1 401.1 %all-gather.23.cloned.1.call-start = ((), (), s32[]{:S(2)}) async-start(), calls=%async_computation.7 | async-start | bytes 6656000 | tf_op jit(solution)/shard_map/all_gather | solution.py:28
  13.7 481.3 %all-gather.19.cloned.1.call-start = ((), (), s32[]{:S(2)}) async-start(), calls=%async_computation.5 | async-start | bytes 6656000 | tf_op jit(solution)/shard_map/all_gather | solution.py:28
  14.3 835.4 %all-reduce.11.cloned.1.call-start = ((), (), s32[]{:S(2)}) async-start(), calls=%async_computation.10 | async-start | bytes 26214400
  17.3 237.6 %copy-start = (bf16[1,2048,640]{1,2,0:T(8,128)(2,1)}, bf16[1,2048,640]{1,2,0:T(8,128)(2,1)S(1)}, u32[]{:S(2)}) copy-start(bf16[1,2048,640]{1,2,0:T(8,128)(2,1)S(1)} %copy.24) | copy-start | bytes 7864324
  17.9 0.9 copy-start.5
  18.8 158.4 %copy-start.7 = (f32[2048]{0:T(1024)}, f32[2048]{0:T(1024)S(1)}, u32[]{:S(2)}) copy-start(f32[2048]{0:T(1024)S(1)} %fusion.86) | copy-start | bytes 24580
  266.9 0.6 copy-start.9
  267.5 146.8 %copy-start.4 = (bf16[2048,640]{0,1:T(8,128)(2,1)S(1)}, bf16[2048,640]{0,1:T(8,128)(2,1)}, u32[]{:S(2)}) copy-start(bf16[2048,640]{0,1:T(8,128)(2,1)} %get-tuple-element.35) | copy-start | bytes 7864324
  539.7 11.0 copy-start.11
  539.7 11.0 copy-start.14
  559.0 22.0 %copy-start.10 = (f32[2048]{0:T(1024)S(1)}, f32[2048]{0:T(1024)}, u32[]{:S(2)}) copy-start(f32[2048]{0:T(1024)} %copy-done.9) | copy-start | bytes 24580
  559.0 22.0 %copy-start.3 = (bf16[1,2048,640]{1,2,0:T(8,128)(2,1)S(1)}, bf16[1,2048,640]{1,2,0:T(8,128)(2,1)}, u32[]{:S(2)}) copy-start(bf16[1,2048,640]{1,2,0:T(8,128)(2,1)} %copy.23) | copy-start | bytes 7864324
  581.0 4.5 copy-start.12
  585.5 25.7 %copy-start.2 = (bf16[2048,640]{0,1:T(8,128)(2,1)}, bf16[2048,640]{0,1:T(8,128)(2,1)S(1)}, u32[]{:S(2)}) copy-start(bf16[2048,640]{0,1:T(8,128)(2,1)S(1)} %fusion.59) | copy-start | bytes 7864324
  585.5 25.7 %copy-start.1 = (bf16[1,2048,640]{1,2,0:T(8,128)(2,1)S(1)}, bf16[1,2048,640]{1,2,0:T(8,128)(2,1)}, u32[]{:S(2)}) copy-start(bf16[1,2048,640]{1,2,0:T(8,128)(2,1)} %copy-done) | copy-start | bytes 7864324
  585.5 25.6 %copy-start.8 = (f32[2048]{0:T(1024)S(1)}, f32[2048]{0:T(1024)}, u32[]{:S(2)}) copy-start(f32[2048]{0:T(1024)} %copy-done.7) | copy-start | bytes 24580
  637.5 13.3 %copy-start.13 = (u32[256]{0:T(256)S(1)}, u32[256]{0:T(256)}, u32[]{:S(2)}) copy-start(u32[256]{0:T(256)} %constant.29) | copy-start | bytes 3076
  637.5 350.7 %reduce-scatter.7.cloned.1.call-start = ((), (), s32[]{:S(2)}) async-start(), calls=%async_computation.8 | async-start | bytes 3328000
  650.7 480.4 %reduce-scatter.9.cloned.1.call-start = ((), (), s32[]{:S(2)}) async-start(), calls=%async_computation.9 | async-start | bytes 3328000
  672.1 511.8 %all-reduce.13.cloned.1.call-start = ((), (), s32[]{:S(2)}) async-start(), calls=%async_computation.11 | async-start | bytes 860160 | tf_op jit(solution)/shard_map/psum | solution.py:31
  685.0 19.9 %copy-start.6 = (f32[2048]{0:T(1024)S(1)}, f32[2048]{0:T(1024)}, u32[]{:S(2)}) copy-start(f32[2048]{0:T(1024)} %copy-done.5) | copy-start | bytes 24580
Sparse Core Ops, SparseCore 0:
  11.2 85.0 all-gather.12
  99.6 77.5 all-gather.14
  179.9 74.9 all-gather.16
  257.4 75.5 all-gather.20
  336.1 78.1 all-gather.22
  417.4 77.5 all-gather.18
  637.6 211.9 all-reduce.10
  853.8 134.3 reduce-scatter.6
  992.4 138.7 reduce-scatter.8
  1134.4 49.5 all-reduce.12
where the time goes:
time: 1210 us; the launch traced here: 1200 us
  waiting for transfers between devices  861 us (71%)
  matrix products  281 us (23%)
  local copies, waits for them, and re-layouts  24 us (2%)
  between operations  15.4 us (1%)
  other arithmetic  14.2 us (1%)
    unnamed x13, waiting for transfers between devices  425 us
    all_gather x6, waiting for transfers between devices, fetched(): lax.all_gather(w[number], 's', axis=0, tiled=True)  394 us
    dot_general x6, matrix products, layer(): up = jnp.dot(a, w['w_up'], preferred_element_type=jnp.float32)  110 us
    dot_general x6, matrix products, layer(): gate = jnp.dot(a, w['w_gate'], preferred_element_type=jnp.float32)  86.3 us
    dot_general x5, matrix products, matmul(): jnp.dot(a, w, preferred_element_type=jnp.float32).astype(jnp.bfloat16)  84.3 us
    psum x1, waiting for transfers between devices, summed(): lax.psum(lax.psum_scatter(term, 's', scatter_dimension=0, tiled=True), 'r')  42.6 us
  transfers between devices with their start and end apart: 10, of which 10 were waited for; matrix products, arithmetic and copies ran while one was open for 14% of the time, Pallas kernels for 0%

commit v1 on v0

v1 whole, which is shorter than its diff:
```python
import functools

import jax
import jax.numpy as jnp
from jax import lax
from jax.experimental import pallas as pl
from jax.experimental.pallas import tpu as pltpu
from jax.sharding import PartitionSpec as P

NAMES = ("w_gate", "w_up", "w_down")
ROWS = 128
NY, NZ = 4, 8


def matmul(a, w):
    return jnp.dot(a, w, preferred_element_type=jnp.float32).astype(jnp.bfloat16)


def normed(h):
    wide = h.astype(jnp.float32)
    scale = lax.rsqrt(jnp.mean(wide**2, -1, keepdims=True) + 1e-6)
    return (wide * scale).astype(jnp.bfloat16)


def layer(h, w):
    a = normed(h)
    gate = jnp.dot(a, w["w_gate"], preferred_element_type=jnp.float32)
    up = jnp.dot(a, w["w_up"], preferred_element_type=jnp.float32)
    return h + matmul((jax.nn.silu(gate) * up).astype(jnp.bfloat16), w["w_down"])


def place(ny, nz):
    s = lax.axis_index("s")
    return s // (2 * nz), lax.rem(s // 2, nz), lax.rem(s, 2)


def greet(peers):
    barrier = pltpu.get_barrier_semaphore()
    for peer in peers:
        pl.semaphore_signal(barrier, inc=1, device_id=peer, device_id_type=pl.DeviceIdType.MESH)
    pl.semaphore_wait(barrier, len(peers))


def remote(src, dst, send, recv, peer):
    return pltpu.make_async_remote_copy(
        src_ref=src, dst_ref=dst, send_sem=send, recv_sem=recv, device_id=peer, device_id_type=pl.DeviceIdType.MESH
    )


def ring(axis, y, z, c, ny, nz):
    n, pos = (ny, y) if axis == "y" else (nz, z)

    def at(k):
        return {"s": ((k * nz + z) if axis == "y" else (y * nz + k)) * 2 + c}

    return n, pos, (at(lax.rem(pos + 1, n)), at(lax.rem(pos + n - 1, n)))


def gather_kernel(ny, nz, w_ref, o_ref, own_sem, pair_send, pair_recv, send1, recv1, send2, recv2):
    rows = w_ref.shape[0]
    half = rows // 2
    y, z, c = place(ny, nz)
    partner = {"s": (y * nz + z) * 2 + (1 - c)}
    peers = [partner, *ring("y", y, z, c, ny, nz)[2], *ring("z", y, z, c, ny, nz)[2]]
    greet(peers)
    own = pltpu.make_async_copy(w_ref, o_ref.at[y, z, c], own_sem)
    own.start()
    own.wait()

    def hand(ref):
        remote(ref, ref, pair_send, pair_recv, partner).start()

    hand(o_ref.at[y, z, c])

    def phase(axis, block, subs, send, recv):
        n, pos, to = ring(axis, y, z, c, ny, nz)
        h = n // 2
        sent = []

        def piece(k, j, which):
            ref = block(k, j)
            return ref if which is None else ref.at[pl.ds(which * half, half)]

        def copy(d, t, j):
            origin = lax.rem(pos + n - t, n) if d == 0 else lax.rem(pos + t, n)
            ref = piece(origin, j, d if t == h - 1 else None)
            return remote(ref, ref, send.at[d, t, j], recv.at[d, t, j], to[d])

        def arrived(d, t, j):
            origin = lax.rem(pos + n - t - 1, n) if d == 0 else lax.rem(pos + t + 1, n)
            ref = piece(origin, j, d if t == h - 1 else None)
            remote(ref, ref, send.at[d, t, j], recv.at[d, t, j], to[d]).wait_recv()
            return ref

        for t in range(h):
            for j in range(subs):
                for d in (0, 1):
                    ref = arrived(d, t - 1, j) if t else None
                    sent.append(copy(d, t, j))
                    sent[-1].start()
                    if t:
                        hand(ref)
        for j in range(subs):
            for d in (0, 1):
                hand(arrived(d, h - 1, j))
        return sent

    @pl.when(c == 0)
    def _():
        sent = phase("y", lambda k, j: o_ref.at[k, z, c], 1, send1, recv1)
        sent += phase("z", lambda k, j: o_ref.at[j, k, c], ny, send2, recv2)
        for copy in sent:
            copy.wait_send()

    @pl.when(c == 1)
    def _():
        sent = phase("z", lambda k, j: o_ref.at[y, k, c], 1, send1, recv1)
        sent += phase("y", lambda k, j: o_ref.at[k, j, c], nz, send2, recv2)
        for copy in sent:
            copy.wait_send()

    remote(o_ref.at[:, :, c], o_ref.at[:, :, c], pair_send, pair_recv, partner).wait_send()
    remote(o_ref.at[:, :, 1 - c], o_ref.at[:, :, 1 - c], pair_send, pair_recv, partner).wait_recv()


def gathered(block, ny=NY, nz=NZ, interpret=False):
    rows, width = block.shape
    dma = pltpu.SemaphoreType.DMA
    return pl.pallas_call(
        functools.partial(gather_kernel, ny, nz),
        out_shape=jax.ShapeDtypeStruct((ny, nz, 2, rows, width), block.dtype),
        in_specs=[pl.BlockSpec(memory_space=pltpu.VMEM)],
        out_specs=pl.BlockSpec(memory_space=pl.ANY),
        scratch_shapes=[dma, dma, dma, dma((2, 4, 1)), dma((2, 4, 1)), dma((2, 4, 8)), dma((2, 4, 8))],
        compiler_params=pltpu.CompilerParams(collective_id=1, has_side_effects=True),
        cost_estimate=pl.CostEstimate(flops=20_000_000_000, bytes_accessed=10_000_000, transcendentals=0),
        name="gather_plane",
    )(block)


def reduce_kernel(nx, ny, nz, g_ref, b_ref, o1_ref, o2_ref, mine, theirs, arrivals1, arrivals2, copies1, copies2, own_sem,
                  pair_send, pair_recv, send1, recv1, send2, recv2, xsend, xrecv):
    rows = b_ref.shape[0]
    half = rows // 2
    tile = min(rows // 2, 64)
    x = lax.axis_index("r")
    y, z, c = place(ny, nz)
    partner = {"s": (y * nz + z) * 2 + (1 - c)}
    planes = [{"r": lax.rem(x + k, nx)} for k in range(1, nx)]
    greet([partner, *ring("y", y, z, c, ny, nz)[2], *ring("z", y, z, c, ny, nz)[2], *planes])
    own = pltpu.make_async_copy(g_ref.at[:, :, c], mine, own_sem)
    own.start()

    def pair(yy, zz, core):
        i = yy * nz + zz
        return remote(g_ref.at[yy, zz, core], theirs.at[yy, zz], pair_send.at[i], pair_recv.at[i], partner)

    def needed(n, pos):
        h = n // 2
        offsets = [h]
        for t in range(1, h):
            offsets += [h - t, n - h + t]
        return [lax.rem(pos + k, n) for k in [*offsets, 0]]

    @pl.when(c == 0)
    def _():
        for k in needed(ny, y):
            for j in range(nz):
                pair(k, j, 1).start()

    @pl.when(c == 1)
    def _():
        for k in needed(nz, z):
            for j in range(ny):
                pair(j, k, 0).start()

    def spread(layer, source, copies):
        return [
            remote(source, copies.at[x], xsend.at[layer, k], xrecv.at[layer, k], peer) for k, peer in enumerate(planes)
        ]

    def add(into, block, first=0, count=rows):
        def body(i, _):
            at = pl.ds(pl.multiple_of(first + i * tile, tile), tile)
            into[at, :] = (into[at, :].astype(jnp.float32) + block[at, :].astype(jnp.float32)).astype(into.dtype)
            return 0

        lax.fori_loop(0, count // tile, body, 0)

    def keep(into, block):
        def body(i, _):
            at = pl.ds(pl.multiple_of(i * tile, tile), tile)
            into[at, :] = block[at, :]
            return 0

        lax.fori_loop(0, rows // tile, body, 0)

    def over_planes(out, copies):
        def body(i, _):
            at = pl.ds(pl.multiple_of(i * tile, tile), tile)
            total = copies[0, at, :].astype(jnp.float32)
            for k in range(1, nx):
                total += copies[k, at, :].astype(jnp.float32)
            out[at, :] = total.astype(out.dtype)
            return 0

        lax.fori_loop(0, rows // tile, body, 0)

    other = spread(1, b_ref, copies2)
    for copy in other:
        copy.start()
    keep(copies2.at[x], b_ref)
    own.wait()

    def both(yy, zz):
        pair(yy, zz, 1 - c).wait_recv()
        add(mine.at[yy, zz], theirs.at[yy, zz])

    def phase(axis, block, subs, ready, arrivals, send, recv):
        n, pos, to = ring(axis, y, z, c, ny, nz)
        h = n // 2
        sent = []

        def rows_of(ref, d, t):
            return ref.at[pl.ds(d * half, half)] if t == 0 else ref

        def arrived(d, t, j, into):
            landed = arrivals.at[d, t * subs + j]
            part = rows_of(landed, d, t)
            remote(part, part, send.at[d, t, j], recv.at[d, t, j], to[d]).wait_recv()
            add(into, landed, d * half if t == 0 else 0, half if t == 0 else rows)

        for t in range(h):
            for j in range(subs):
                for d in (0, 1):
                    k = lax.rem(pos + h - t, n) if d == 0 else lax.rem(pos + n - h + t, n)
                    if t or d == 0:
                        ready(k, j)
                    if t:
                        arrived(d, t - 1, j, block(k, j))
                    sent.append(
                        remote(
                            rows_of(block(k, j), d, t), rows_of(arrivals.at[d, t * subs + j], d, t),
                            send.at[d, t, j], recv.at[d, t, j], to[d],
                        )
                    )
                    sent[-1].start()
        for j in range(subs):
            ready(pos, j)
            for d in (0, 1):
                arrived(d, h - 1, j, block(pos, j))
        return sent

    def done(k, j):
        pass

    @pl.when(c == 0)
    def _():
        sent = phase("z", lambda k, j: mine.at[j, k], ny, lambda k, j: both(j, k), arrivals1, send1, recv1)
        sent += phase("y", lambda k, j: mine.at[k, z], 1, done, arrivals2, send2, recv2)
        for copy in sent:
            copy.wait_send()

    @pl.when(c == 1)
    def _():
        sent = phase("y", lambda k, j: mine.at[k, j], nz, lambda k, j: both(k, j), arrivals1, send1, recv1)
        sent += phase("z", lambda k, j: mine.at[y, k], 1, done, arrivals2, send2, recv2)
        for copy in sent:
            copy.wait_send()

    last = spread(0, mine.at[y, z], copies1)
    for copy in last:
        copy.start()
    keep(copies1.at[x], mine.at[y, z])
    for copy in other:
        copy.wait()
    over_planes(o2_ref, copies2)
    for copy in last:
        copy.wait()
    over_planes(o1_ref, copies1)
    for yy in range(ny):
        for zz in range(nz):
            pair(yy, zz, 1 - c).wait_send()


def reduced(grads, block, nx, ny=NY, nz=NZ):
    rows, width = block.shape
    dma = pltpu.SemaphoreType.DMA
    vmem = lambda *lead: pltpu.VMEM((*lead, rows, width), jnp.bfloat16)
    one = jax.ShapeDtypeStruct((rows, width), jnp.bfloat16)
    return pl.pallas_call(
        functools.partial(reduce_kernel, nx, ny, nz),
        out_shape=(one, one),
        in_specs=[pl.BlockSpec(memory_space=pl.ANY), pl.BlockSpec(memory_space=pltpu.VMEM)],
        out_specs=(pl.BlockSpec(memory_space=pltpu.VMEM),) * 2,
        scratch_shapes=[
            vmem(ny, nz), vmem(ny, nz), vmem(2, ny * nz // 2), vmem(2, max(ny, nz) // 2), vmem(nx), vmem(nx),
            dma, dma((ny * nz,)), dma((ny * nz,)),
            dma((2, 4, 8)), dma((2, 4, 8)), dma((2, 4, 1)), dma((2, 4, 1)), dma((2, max(nx - 1, 1))), dma((2, max(nx - 1, 1))),
        ],
        compiler_params=pltpu.CompilerParams(collective_id=2, has_side_effects=True, vmem_limit_bytes=40 * 2**20),
        cost_estimate=pl.CostEstimate(flops=40_000_000_000, bytes_accessed=20_000_000, transcendentals=0),
        name="reduce_all",
    )(grads, block)


def solution(mesh):
    nx = mesh.shape["r"]
    shards = mesh.shape["s"]

    def packed(weights, number):
        return jnp.concatenate([w[number].reshape(-1, 640) for w in weights], axis=0)

    def padded(block):
        return jnp.pad(block, ((0, ROWS - block.shape[0]), (0, 0)))

    def matrices(blocks):
        gate, up, down = (blocks[:, 40 * i : 40 * i + 40] for i in range(3))
        return {"w_gate": gate.reshape(640, 2560), "w_up": up.reshape(640, 2560), "w_down": down.reshape(2560, 640)}

    def terms(by_w, pad):
        parts = [by_w[name].reshape(shards, 40, 640) for name in NAMES]
        if pad:
            parts.append(jnp.zeros((shards, ROWS - 120, 640), jnp.bfloat16))
        return jnp.concatenate(parts, axis=1)

    def step(x, dy, *weights):
        blocks = lax.all_gather(packed(weights, 1), "s", axis=0, tiled=True)
        first = gathered(padded(packed(weights, 0))).reshape(shards, ROWS, 640)
        h0 = x[0]
        w0 = matrices(first)
        h1 = layer(h0, w0)
        w1 = matrices(blocks.reshape(shards, 120, 640))
        _, back = jax.vjp(lambda w, h: layer(h, w), w1, h1)
        by_w, by_h = back(dy[0])
        second = lax.psum_scatter(terms(by_w, False).reshape(-1, 640), "s", scatter_dimension=0, tiled=True)
        w0, h0, by_h = lax.optimization_barrier((w0, h0, by_h))
        _, back = jax.vjp(lambda w, h: layer(h, w), w0, h0)
        by_w, by_x = back(by_h)
        one, two = reduced(terms(by_w, True).reshape(NY, NZ, 2, ROWS, 640), padded(second), nx)
        both = jnp.stack([one, two])
        mine = [both[:, :40].reshape(2, 10, 2560), both[:, 40:80].reshape(2, 10, 2560), both[:, 80:120]]
        return (by_x[None], *mine)

    states, cut = P(("rep", "r", "s"), None, None), P(None, "s", None)
    return jax.shard_map(
        step,
        mesh=mesh,
        in_specs=(states, states) + (cut,) * 3,
        out_specs=(states,) + (P("rep", "s", None),) * 3,
        check_vma=False,
    )
```

time: 1210 us -> 547 us (0.45)
  waiting for transfers between devices: 861 us -> 0.06 us
  Pallas kernels: 0 us -> 122 us
  local copies, waits for them, and re-layouts: 24 us -> 85.8 us
  other arithmetic: 14.2 us -> 28.3 us
    unnamed x13 -> x3, waiting for transfers between devices: 425 us -> 0.03 us
    all_gather x6 -> x1, waiting for transfers between devices: 394 us -> 0.02 us  [step(): blocks = lax.all_gather(packed(weights, 1), 's', axis=0, tiled=True)]
    pallas_call x0 -> x2, Pallas kernels: none -> 122 us  [the longest x1 66 us: gathered(): pl.pallas_call(functools.partial(gather_kernel, ny, nz), out_shape=jax.Sh...]
    psum x1 -> x0, waiting for transfers between devices: 42.6 us -> none  [summed(): lax.psum(lax.psum_scatter(term, 's', scatter_dimension=0, tiled=True), 'r')]
    reshape x0 -> x8, local copies, waits for them, and re-layouts: none -> 34 us  [the longest x2 12.5 us: matrices(): gate.reshape(640, 2560)]
    dot_general x6 -> x7, matrix products: 86.3 us -> 115 us  [layer(): gate = jnp.dot(a, w['w_gate'], preferred_element_type=jnp.float32)]
    dot_general x6, matrix products: 110 us -> 85.6 us  [layer(): up = jnp.dot(a, w['w_up'], preferred_element_type=jnp.float32)]
    concatenate x0 -> x4, other arithmetic: none -> 16.2 us  [the longest x2 14.9 us: terms(): return jnp.concatenate(parts, axis=1)]
  transfers between devices with their start and end apart: 10 -> 2, of which waited for: 10 -> 0; matrix products, arithmetic and copies ran while one was open for 14% -> 41% of each run, Pallas kernels for 0% -> 12%
where the time goes in v1:
time: 547 us; the launch traced here: 542 us
  matrix products  291 us (53%)
  Pallas kernels  122 us (22%)
  local copies, waits for them, and re-layouts  85.8 us (16%)
  other arithmetic  28.3 us (5%)
  between operations  14.5 us (3%)
    dot_general x7, matrix products, layer(): gate = jnp.dot(a, w['w_gate'], preferred_element_type=jnp.float32)  115 us
    dot_general x5, matrix products, matmul(): jnp.dot(a, w, preferred_element_type=jnp.float32).astype(jnp.bfloat16)  90.6 us
    dot_general x6, matrix products, layer(): up = jnp.dot(a, w['w_up'], preferred_element_type=jnp.float32)  85.6 us
    pallas_call x1, Pallas kernels, gathered(): pl.pallas_call(functools.partial(gather_kernel, ny, nz), out_shape=jax.Sh...  66 us
    pallas_call x1, Pallas kernels, reduced(): pl.pallas_call(functools.partial(reduce_kernel, nx, ny, nz), out_shape=(o...  56 us
    unnamed x41, local copies, waits for them, and re-layouts  20.8 us
    concatenate x2, other arithmetic, terms(): return jnp.concatenate(parts, axis=1)  14.9 us
    slice x2, local copies, waits for them, and re-layouts, matrices(): gate, up, down = (blocks[:, 40 * i:40 * i + 40] for i in range(3))  13.1 us
  transfers between devices with their start and end apart: 2, of which 0 were waited for; matrix products, arithmetic and copies ran while one was open for 41% of the time, Pallas kernels for 12%

profile of v1, /device:TPU:1, one launch (start us, length us, event | category | flops | bytes accessed | tf_op | source)
XLA Modules:
  0.0 542.1 jit_solution(17606882394882772709)
XLA Ops:
  7.2 0.8 slice_bitcast_fusion
  8.1 1.4 slice_reduce_fusion.1
  9.5 1.4 slice_reduce_fusion
  11.0 0.7 pad_maximum_fusion.1
  11.9 3.0 copy.21
  14.9 5.1 copy.22
  20.0 0.7 fusion.60.w_ref
  20.7 66.0 %gather_plane.1 = bf16[4,8,2,128,640]{4,3,2,1,0:T(8,128)(2,1)} custom-call(bf16[128,640]{1,0:T(8,128)(2,1)} %fusion.60.w_ref), custom_call_target="tpu_custom_call" | custom-call | flops 20000000000 | bytes 10000000 | tf_op jit(solution)/shard_map/gather_plane/pallas_call | solution.py:129
  86.7 7.0 %fusion.70 = (bf16[64,40,640]{2,1,0:T(8,128)(2,1)}, bf16[64,40,640]{2,1,0:T(8,128)(2,1)}, bf16[64,40,640]{2,1,0:T(8,128)(2,1)}) fusion(bf16[64,128,640]{2,1,0:T(8,128)(2,1)} %bitcast.75), kind=kLoop, calls=%fused_computation.100 | loop fusion | bytes 19660800 | tf_op jit(solution)/shard_map/slice | solution.py:318
  93.7 6.2 %reshape.120 = bf16[640,2560]{1,0:T(8,128)(2,1)} reshape(bf16[64,40,640]{2,1,0:T(8,128)(2,1)} %get-tuple-element.34) | data formatting | bytes 6553600 | tf_op jit(solution)/shard_map/reshape | solution.py:319
  99.9 6.2 %reshape.119 = bf16[640,2560]{1,0:T(8,128)(2,1)} reshape(bf16[64,40,640]{2,1,0:T(8,128)(2,1)} %get-tuple-element.35) | data formatting | bytes 6553600 | tf_op jit(solution)/shard_map/reshape | solution.py:319
  107.3 14.7 %fusion.54 = f32[2048,2560]{1,0:T(8,128)} fusion(bf16[640,2560]{1,0:T(8,128)(2,1)} %reshape.119, bf16[1,2048,640]{2,1,0:T(8,128)(2,1)} %param.5, f32[2048]{0:T(1024)S(1)} %add_rsqrt_fusion), kind=kOutput, calls=%fused_computation.75 | convolution fusion | flops 6714818560 | bytes 26877952 | tf_op jit(solution)/shard_map/dot_general | solution.py:27
  122.1 22.4 %fusion.18 = (f32[2048]{0:T(1024)S(1)}, bf16[2048,640]{0,1:T(8,128)(2,1)}) fusion(bf16[2560,640]{1,0:T(8,128)(2,1)} %bitcast.76, f32[2048,2560]{1,0:T(8,128)} %fusion.54, bf16[640,2560]{1,0:T(8,128)(2,1)} %reshape.120, bf16[1,2048,640]{2,1,0:T(8,128)(2,1)} %param.5, f32[2048]{0:T(1024)S(1)} %add_rsqrt_fusion, bf16[1,2048,640]{1,2,0:T(8,128)(2,1)S(1)} %copy.21), kind=kOutput, calls=%fused_computation.43 | convolution fusion | flops 13467645952 | bytes 35405824 | tf_op jit(solution)/shard_map/dot_general | solution.py:16
  145.1 6.1 %fusion.71 = (bf16[64,40,640]{2,1,0:T(8,128)(2,1)}, bf16[64,40,640]{2,1,0:T(8,128)(2,1)S(1)}, bf16[64,40,640]{2,1,0:T(8,128)(2,1)}) fusion(bf16[64,120,640]{2,1,0:T(8,128)(2,1)} %bitcast.74), kind=kLoop, calls=%fused_computation.101 | loop fusion | bytes 19660800 | tf_op jit(solution)/shard_map/slice | solution.py:318
  151.2 6.2 %reshape.122 = bf16[640,2560]{1,0:T(8,128)(2,1)} reshape(bf16[64,40,640]{2,1,0:T(8,128)(2,1)} %get-tuple-element.37) | data formatting | bytes 6553600 | tf_op jit(solution)/shard_map/reshape | solution.py:319
  157.5 3.7 reshape.124
  161.2 13.6 %convolution_convert_fusion = bf16[2560,2048]{0,1:T(8,128)(2,1)} fusion(bf16[2560,640]{1,0:T(8,128)(2,1)} %bitcast.79, bf16[1,2048,640]{2,1,0:T(8,128)(2,1)} %param.6), kind=kOutput, calls=%fused_computation.22 | convolution fusion | flops 6716129280 | bytes 16384000 | tf_op jit(solution)/shard_map/transpose(jvp())/dot_general | solution.py:16
  174.9 11.4 %fusion.48 = f32[2048,2560]{1,0:T(8,128)} fusion(bf16[640,2560]{1,0:T(8,128)(2,1)S(1)} %copy-done.9, bf16[2048,640]{0,1:T(8,128)(2,1)S(1)} %copy-done.10, f32[2048]{0:T(1024)S(1)} %fusion.61), kind=kOutput, calls=%fused_computation.73 | convolution fusion | flops 6714818560 | bytes 26877952 | tf_op jit(solution)/shard_map/jvp()/dot_general | solution.py:28
  186.3 28.2 %fusion.1 = (bf16[2048,2560]{1,0:T(8,128)(2,1)}, f32[2048,2560]{1,0:T(8,128)}) fusion(f32[2048,2560]{1,0:T(8,128)} %fusion.48, bf16[2560,2048]{0,1:T(8,128)(2,1)} %convolution_convert_fusion, bf16[640,2560]{1,0:T(8,128)(2,1)S(1)} %copy-done.8, bf16[2048,640]{0,1:T(8,128)(2,1)} %get-tuple-element.46, f32[2048]{0:T(1024)S(1)} %fusion.61), kind=kOutput, calls=%fused_computation.5 | convolution fusion | flops 6777733120 | bytes 68820992 | tf_op jit(solution)/shard_map/jvp()/dot_general | solution.py:27
  214.5 20.3 %fusion.24 = bf16[2560,640]{1,0:T(8,128)(2,1)} fusion(f32[2048,2560]{1,0:T(8,128)} %fusion.48, bf16[1,2048,640]{2,1,0:T(8,128)(2,1)} %param.6, f32[2048,2560]{1,0:T(8,128)} %get-tuple-element.48), kind=kOutput, calls=%fused_computation.51 | convolution fusion | flops 6743982080 | bytes 47841280 | tf_op jit(solution)/shard_map/transpose(jvp())/dot_general | solution.py:16
  234.8 15.9 %fusion.30 = bf16[2048,640]{0,1:T(8,128)(2,1)} fusion(bf16[640,2560]{1,0:T(8,128)(2,1)} %reshape.124, bf16[2560,2048]{0,1:T(8,128)(2,1)} %convolution_convert_fusion, f32[2048,2560]{1,0:T(8,128)} %get-tuple-element.48), kind=kOutput, calls=%fused_computation.59 | convolution fusion | flops 6743654400 | bytes 37355520 | tf_op jit(solution)/shard_map/transpose(jvp())/dot_general | solution.py:28
  250.7 15.4 %fusion.27 = bf16[640,2560]{1,0:T(8,128)(2,1)} fusion(bf16[2560,2048]{0,1:T(8,128)(2,1)} %convolution_convert_fusion, bf16[2048,640]{0,1:T(8,128)(2,1)S(1)} %copy-done.11, f32[2048]{0:T(1024)S(1)} %fusion.61, f32[2048,2560]{1,0:T(8,128)} %get-tuple-element.48), kind=kOutput, calls=%fused_computation.54 | convolution fusion | flops 6747914240 | bytes 37363712 | tf_op jit(solution)/shard_map/transpose(jvp())/dot_general | solution.py:28
  266.2 11.1 %convolution_convert_fusion.2 = bf16[640,2560]{1,0:T(8,128)(2,1)} fusion(bf16[2048,2560]{1,0:T(8,128)(2,1)} %get-tuple-element.47, bf16[2048,640]{0,1:T(8,128)(2,1)S(1)} %copy-done.11, f32[2048]{0:T(1024)S(1)} %fusion.61), kind=kOutput, calls=%fused_computation.55 | convolution fusion | flops 6714818560 | bytes 16392192 | tf_op jit(solution)/shard_map/transpose(jvp())/dot_general | solution.py:27
  277.2 11.0 %fusion.20 = (f32[2048]{0:T(1024)S(1)}, bf16[2048,640]{0,1:T(8,128)(2,1)}) fusion(bf16[2048,640]{0,1:T(8,128)(2,1)S(1)} %copy-done.11, bf16[2048,640]{0,1:T(8,128)(2,1)S(1)} %copy-done.17, bf16[2048,2560]{1,0:T(8,128)(2,1)} %get-tuple-element.47, bf16[640,2560]{1,0:T(8,128)(2,1)S(1)} %copy-done.8), kind=kOutput, calls=%fused_computation.45 | convolution fusion | flops 6717437952 | bytes 21635072 | tf_op jit(solution)/shard_map/transpose(jvp())/dot_general | solution.py:27
  288.2 5.1 reshape.125
  293.4 6.3 %reshape.126 = bf16[64,40,640]{2,1,0:T(8,128)(2,1)} reshape(bf16[640,2560]{1,0:T(8,128)(2,1)} %fusion.27) | data formatting | bytes 6553600 | tf_op jit(solution)/shard_map/reshape | solution.py:322
  299.7 7.0 %fusion.34 = bf16[2048,640]{0,1:T(8,128)(2,1)} fusion(bf16[2048,640]{0,1:T(8,128)(2,1)} %get-tuple-element.46, bf16[2048,640]{0,1:T(8,128)(2,1)} %get-tuple-element.50, bf16[1,2048,640]{1,2,0:T(8,128)(2,1)} %copy.22, f32[2048]{0:T(1024)S(1)} %multiply_multiply_fusion.1, f32[2048]{0:T(1024)S(1)} %fusion.61), kind=kLoop, calls=%fused_computation.65 | loop fusion | flops 9175040 | bytes 10502144 | tf_op jit(solution)/shard_map/transpose(jvp())/add_any | solution.py:20
  306.7 5.3 pad_maximum_fusion
  312.0 1.7 copy-done.2
  314.8 13.5 %convolution_convert_fusion.1 = bf16[2048,2560]{1,0:T(8,128)(2,1)} fusion(bf16[2048,640]{0,1:T(8,128)(2,1)} %fusion.34, bf16[2560,640]{1,0:T(8,128)(2,1)} %bitcast.77), kind=kOutput, calls=%fused_computation.23 | convolution fusion | flops 6716129280 | bytes 16384000 | tf_op jit(solution)/shard_map/transpose(jvp())/dot_general | solution.py:16
  328.4 11.3 %fusion.42 = f32[2048,2560]{1,0:T(8,128)} fusion(bf16[640,2560]{1,0:T(8,128)(2,1)S(1)} %copy-done.7, bf16[2048,640]{0,1:T(8,128)(2,1)S(1)} %bitcast.67, f32[2048]{0:T(1024)S(1)} %fusion.62), kind=kOutput, calls=%fused_computation.71 | convolution fusion | flops 6714818560 | bytes 26877952 | tf_op jit(solution)/shard_map/jvp()/dot_general | solution.py:28
  339.7 27.8 %fusion.3 = (bf16[2048,2560]{1,0:T(8,128)(2,1)}, f32[2048,2560]{1,0:T(8,128)}) fusion(f32[2048,2560]{1,0:T(8,128)} %fusion.42, bf16[2048,2560]{1,0:T(8,128)(2,1)} %convolution_convert_fusion.1, bf16[640,2560]{1,0:T(8,128)(2,1)} %reshape.119, bf16[2048,640]{0,1:T(8,128)(2,1)S(1)} %bitcast.68, f32[2048]{0:T(1024)S(1)} %fusion.62), kind=kOutput, calls=%fused_computation.7 | convolution fusion | flops 6777733120 | bytes 68820992 | tf_op jit(solution)/shard_map/jvp()/dot_general | solution.py:27
  367.4 16.1 %fusion.29 = bf16[2048,640]{0,1:T(8,128)(2,1)} fusion(bf16[640,2560]{1,0:T(8,128)(2,1)} %reshape.120, bf16[2048,2560]{1,0:T(8,128)(2,1)} %convolution_convert_fusion.1, f32[2048,2560]{1,0:T(8,128)} %get-tuple-element.52), kind=kOutput, calls=%fused_computation.58 | convolution fusion | flops 6743654400 | bytes 37355520 | tf_op jit(solution)/shard_map/transpose(jvp())/dot_general | solution.py:28
  383.6 10.9 %convolution_convert_fusion.3 = bf16[640,2560]{1,0:T(8,128)(2,1)} fusion(bf16[2048,2560]{1,0:T(8,128)(2,1)} %get-tuple-element.51, bf16[2048,640]{0,1:T(8,128)(2,1)S(1)} %bitcast.69, f32[2048]{0:T(1024)S(1)} %fusion.62), kind=kOutput, calls=%fused_computation.56 | convolution fusion | flops 6714818560 | bytes 16392192 | tf_op jit(solution)/shard_map/transpose(jvp())/dot_general | solution.py:27
  394.4 6.2 %concatenate.21 = bf16[4,8,2,40,640]{4,3,2,1,0:T(8,128)(2,1)} reshape(bf16[640,2560]{1,0:T(8,128)(2,1)} %convolution_convert_fusion.3) | data formatting | bytes 6553600 | tf_op jit(solution)/shard_map/concatenate | solution.py:325
  400.7 11.4 %fusion.23 = (f32[2048]{0:T(1024)S(1)}, bf16[2048,640]{0,1:T(8,128)(2,1)S(1)}) fusion(bf16[2048,640]{0,1:T(8,128)(2,1)S(1)} %bitcast.70, bf16[2048,640]{0,1:T(8,128)(2,1)} %fusion.29, bf16[2048,2560]{1,0:T(8,128)(2,1)} %get-tuple-element.51, bf16[640,2560]{1,0:T(8,128)(2,1)} %reshape.119), kind=kOutput, calls=%fused_computation.48 | convolution fusion | flops 6717437952 | bytes 21635072 | tf_op jit(solution)/shard_map/transpose(jvp())/dot_general | solution.py:27
  412.2 3.3 fusion.33
  415.4 4.4 copy.24
  419.8 15.4 %fusion.26 = bf16[640,2560]{1,0:T(8,128)(2,1)} fusion(bf16[2048,2560]{1,0:T(8,128)(2,1)} %convolution_convert_fusion.1, bf16[2048,640]{0,1:T(8,128)(2,1)S(1)} %bitcast.72, f32[2048]{0:T(1024)S(1)} %fusion.62, f32[2048,2560]{1,0:T(8,128)} %get-tuple-element.52), kind=kOutput, calls=%fused_computation.53 | convolution fusion | flops 6747914240 | bytes 37363712 | tf_op jit(solution)/shard_map/transpose(jvp())/dot_general | solution.py:28
  435.2 6.2 %concatenate.22 = bf16[4,8,2,40,640]{4,3,2,1,0:T(8,128)(2,1)} reshape(bf16[640,2560]{1,0:T(8,128)(2,1)} %fusion.26) | data formatting | bytes 6553600 | tf_op jit(solution)/shard_map/concatenate | solution.py:325
  441.5 20.7 %fusion.25 = bf16[2560,640]{1,0:T(8,128)(2,1)} fusion(bf16[2048,640]{0,1:T(8,128)(2,1)} %fusion.34, f32[2048,2560]{1,0:T(8,128)} %fusion.42, f32[2048,2560]{1,0:T(8,128)} %get-tuple-element.52), kind=kOutput, calls=%fused_computation.52 | convolution fusion | flops 6743982080 | bytes 47841280 | tf_op jit(solution)/shard_map/transpose(jvp())/dot_general | solution.py:16
  462.2 9.6 %maximum_maximum_fusion.g_ref = bf16[4,8,2,128,640]{4,3,2,1,0:T(8,128)(2,1)} fusion(bf16[4,8,2,40,640]{4,3,2,1,0:T(8,128)(2,1)} %bitcast.80, bf16[4,8,2,40,640]{4,3,2,1,0:T(8,128)(2,1)} %concatenate.22, bf16[4,8,2,40,640]{4,3,2,1,0:T(8,128)(2,1)S(1)} %copy-done.4, bf16[128]{0:T(256)(128)(2,1)S(1)} %copy-done.16), kind=kLoop, calls=%fused_computation.26 | loop fusion | flops 41943040 | bytes 20316416 | tf_op jit(solution)/shard_map/concatenate | solution.py:325
  471.8 0.9 pad.8.b_ref
  472.7 4.0 copy-done
  476.7 56.0 %reduce_all.1 = (bf16[128,640]{1,0:T(8,128)(2,1)S(1)}, bf16[128,640]{1,0:T(8,128)(2,1)S(1)}) custom-call(bf16[4,8,2,128,640]{4,3,2,1,0:T(8,128)(2,1)S(1)} %copy-done, bf16[128,640]{1,0:T(8,128)(2,1)S(1)} %pad.8.b_ref), custom_call_target="tpu_custom_call" | custom-call | flops 40000000000 | bytes 20000000 | tf_op jit(solution)/shard_map/reduce_all/pallas_call | solution.py:291
  532.7 0.7 pad_maximum_fusion.2
  533.4 0.7 copy.26
  534.2 0.7 copy.25
  (55 shorter events, 3.4 us)
Async XLA Ops:
  7.2 137.4 %all-gather.2.cloned.1.call-start = ((), (), s32[]{:S(2)}) async-start(), calls=%async_computation.1 | async-start | bytes 9984000 | tf_op jit(solution)/shard_map/all_gather | solution.py:328
  11.8 460.0 %reduce-scatter.4.cloned.1.call-start = ((), (), s32[]{:S(2)}) async-start(), calls=%async_computation.2 | async-start | bytes 9984000
  14.9 107.2 %copy-start.1 = (bf16[1,2048,640]{1,2,0:T(8,128)(2,1)}, bf16[1,2048,640]{1,2,0:T(8,128)(2,1)S(1)}, u32[]{:S(2)}) copy-start(bf16[1,2048,640]{1,2,0:T(8,128)(2,1)S(1)} %copy.21) | copy-start | bytes 7864324
  144.5 0.6 copy-start.14
  161.2 13.6 %copy-start.9 = (bf16[640,2560]{1,0:T(8,128)(2,1)S(1)}, bf16[640,2560]{1,0:T(8,128)(2,1)}, u32[]{:S(2)}) copy-start(bf16[640,2560]{1,0:T(8,128)(2,1)} %reshape.124) | copy-start | bytes 9830404
  161.2 13.6 %copy-start.10 = (bf16[2048,640]{0,1:T(8,128)(2,1)S(1)}, bf16[2048,640]{0,1:T(8,128)(2,1)}, u32[]{:S(2)}) copy-start(bf16[2048,640]{0,1:T(8,128)(2,1)} %get-tuple-element.46) | copy-start | bytes 7864324
  174.8 11.4 %copy-start.8 = (bf16[640,2560]{1,0:T(8,128)(2,1)S(1)}, bf16[640,2560]{1,0:T(8,128)(2,1)}, u32[]{:S(2)}) copy-start(bf16[640,2560]{1,0:T(8,128)(2,1)} %reshape.122) | copy-start | bytes 9830404
  234.8 15.9 %copy-start.11 = (bf16[2048,640]{0,1:T(8,128)(2,1)S(1)}, bf16[2048,640]{0,1:T(8,128)(2,1)}, u32[]{:S(2)}) copy-start(bf16[2048,640]{0,1:T(8,128)(2,1)} %get-tuple-element.46) | copy-start | bytes 7864324
  266.2 11.1 %copy-start.17 = (bf16[2048,640]{0,1:T(8,128)(2,1)S(1)}, bf16[2048,640]{0,1:T(8,128)(2,1)}, u32[]{:S(2)}) copy-start(bf16[2048,640]{0,1:T(8,128)(2,1)} %fusion.30) | copy-start | bytes 7864324
  288.2 5.1 copy-start.15
  299.7 7.0 %copy-start.3 = (bf16[64,40,640]{2,1,0:T(8,128)(2,1)S(1)}, bf16[64,40,640]{2,1,0:T(8,128)(2,1)}, u32[]{:S(2)}) copy-start(bf16[64,40,640]{2,1,0:T(8,128)(2,1)} %reshape.126) | copy-start | bytes 9830404
  299.7 7.0 %copy-start.6 = (bf16[2560,640]{1,0:T(8,128)(2,1)S(1)}, bf16[2560,640]{1,0:T(8,128)(2,1)}, u32[]{:S(2)}) copy-start(bf16[2560,640]{1,0:T(8,128)(2,1)} %fusion.24) | copy-start | bytes 9830404
  311.9 1.7 copy-start.2
  314.2 0.6 copy-start.12
  314.8 13.5 %copy-start.7 = (bf16[640,2560]{1,0:T(8,128)(2,1)S(1)}, bf16[640,2560]{1,0:T(8,128)(2,1)}, u32[]{:S(2)}) copy-start(bf16[640,2560]{1,0:T(8,128)(2,1)} %reshape.120) | copy-start | bytes 9830404
  400.7 11.4 %copy-start.13 = (f32[2048]{0:T(1024)S(1)}, f32[2048]{0:T(1024)}, u32[]{:S(2)}) copy-start(f32[2048]{0:T(1024)} %copy-done.12) | copy-start | bytes 24580
  400.7 11.5 %copy-start.5 = (bf16[2048,640]{0,1:T(8,128)(2,1)S(1)}, bf16[2048,640]{0,1:T(8,128)(2,1)}, u32[]{:S(2)}) copy-start(bf16[2048,640]{0,1:T(8,128)(2,1)} %fusion.34) | copy-start | bytes 7864324
  441.5 20.7 %copy-start.4 = (bf16[4,8,2,40,640]{4,3,2,1,0:T(8,128)(2,1)S(1)}, bf16[4,8,2,40,640]{4,3,2,1,0:T(8,128)(2,1)}, u32[]{:S(2)}) copy-start(bf16[4,8,2,40,640]{4,3,2,1,0:T(8,128)(2,1)} %concatenate.21) | copy-start | bytes 9830404
  441.5 20.7 %copy-start.16 = (bf16[128]{0:T(256)(128)(2,1)S(1)}, bf16[128]{0:T(256)(128)(2,1)}, u32[]{:S(2)}) copy-start(bf16[128]{0:T(256)(128)(2,1)} %pad.17.clone) | copy-start | bytes 772
  472.7 4.0 copy-start
Sparse Core Ops, SparseCore 0:
  11.9 92.2 all-gather.1
  312.1 140.3 reduce-scatter.3

commit v2 on v0

v2 whole, which is shorter than its diff:
```python
import functools

import jax
import jax.numpy as jnp
from jax import lax
from jax.experimental import pallas as pl
from jax.experimental.pallas import tpu as pltpu
from jax.sharding import PartitionSpec as P

NY, NZ = 4, 8
EDGE = 16


def scale_of(wide):
    return lax.rsqrt(jnp.mean(wide**2, -1, keepdims=True) + 1e-6)


def dot(a, b):
    return jnp.dot(a, b, preferred_element_type=jnp.float32)


def dot_t(a, b):
    return lax.dot_general(a, b, (((1,), (1,)), ((), ())), preferred_element_type=jnp.float32)


def tiles(count, size, body):
    def run(i, _):
        body(pl.ds(pl.multiple_of(i * size, size), size))
        return 0

    lax.fori_loop(0, count // size, run, 0)


def forward_kernel(steps, tile, h_ref, g_ref, u_ref, d_ref, y_ref, a_ref, total):
    q = pl.program_id(0)
    tokens = h_ref.shape[0]

    @pl.when(q == 0)
    def _():
        def start(at):
            wide = h_ref[at, :].astype(jnp.float32)
            a_ref[at, :] = (wide * scale_of(wide)).astype(jnp.bfloat16)
            total[at, :] = jnp.zeros((tile, h_ref.shape[1]), jnp.float32)

        tiles(tokens, tile, start)

    def main(at):
        a = a_ref[at, :]
        gate, up = dot(a, g_ref[...]), dot(a, u_ref[...])
        act = (gate * jax.nn.sigmoid(gate) * up).astype(jnp.bfloat16)
        total[at, :] += dot(act, d_ref[...])

    tiles(tokens, tile, main)

    @pl.when(q == steps - 1)
    def _():
        def end(at):
            y_ref[at, :] = h_ref[at, :] + total[at, :].astype(jnp.bfloat16)

        tiles(tokens, tile, end)


def forward(h, number, both, down, tile=512):
    tokens, d = h.shape
    steps = both.shape[2] // d
    whole = pl.BlockSpec((tokens, d), lambda q: (0, 0))
    gate_at = pl.BlockSpec((None, d, d), lambda q: (2 * number, 0, q))
    up_at = pl.BlockSpec((None, d, d), lambda q: (2 * number + 1, 0, q))
    down_at = pl.BlockSpec((None, d, d), lambda q: (number, q, 0))
    return pl.pallas_call(
        functools.partial(forward_kernel, steps, tile),
        grid=(steps,),
        out_shape=jax.ShapeDtypeStruct((tokens, d), jnp.bfloat16),
        in_specs=[whole, gate_at, up_at, down_at],
        out_specs=whole,
        scratch_shapes=[pltpu.VMEM((tokens, d), jnp.bfloat16), pltpu.VMEM((tokens, d), jnp.float32)],
        compiler_params=pltpu.CompilerParams(dimension_semantics=("arbitrary",), vmem_limit_bytes=48 * 2**20),
        cost_estimate=pl.CostEstimate(flops=20_000_000_000, bytes_accessed=15_000_000, transcendentals=5_000_000),
        name="layer_forward",
    )(h, both, both, down)


def backward_kernel(steps, tile, h_ref, dy_ref, g_ref, u_ref, d_ref, by_both, by_d, by_h,
                    a_ref, at_ref, dyt_ref, act_ref, dgate_ref, dup_ref, total_g, total_u):
    q = pl.program_id(0)
    tokens, d = h_ref.shape

    @pl.when(q == 0)
    def _():
        def start(at):
            wide = h_ref[at, :].astype(jnp.float32)
            a = (wide * scale_of(wide)).astype(jnp.bfloat16)
            a_ref[at, :] = a
            at_ref[:, at] = a.T
            dyt_ref[:, at] = dy_ref[at, :].T
            total_g[at, :] = jnp.zeros((tile, d), jnp.float32)
            total_u[at, :] = jnp.zeros((tile, d), jnp.float32)

        tiles(tokens, tile, start)

    def main(at):
        a = a_ref[at, :]
        gate, up = dot(a, g_ref[...]), dot(a, u_ref[...])
        dact = dot_t(dy_ref[at, :], d_ref[...]).astype(jnp.bfloat16).astype(jnp.float32)
        s = jax.nn.sigmoid(gate)
        silu = gate * s
        act_ref[at, :] = (silu * up).astype(jnp.bfloat16)
        dup = (dact * silu).astype(jnp.bfloat16)
        dgate = (dact * up * (s + silu * (1.0 - s))).astype(jnp.bfloat16)
        dup_ref[at, :] = dup
        dgate_ref[at, :] = dgate
        total_g[at, :] += dot_t(dgate, g_ref[...])
        total_u[at, :] += dot_t(dup, u_ref[...])

    tiles(tokens, tile, main)

    by_d[...] = dot(dyt_ref[...], act_ref[...]).T.astype(jnp.bfloat16)
    by_both[0] = dot(at_ref[...], dgate_ref[...]).astype(jnp.bfloat16)
    by_both[1] = dot(at_ref[...], dup_ref[...]).astype(jnp.bfloat16)

    @pl.when(q == steps - 1)
    def _():
        def end(at):
            wide = h_ref[at, :].astype(jnp.float32)
            scale = scale_of(wide)
            da = (total_g[at, :].astype(jnp.bfloat16) + total_u[at, :].astype(jnp.bfloat16)).astype(jnp.float32)
            along = jnp.sum(da * wide, -1, keepdims=True) * (scale * scale * scale) * (1.0 / d)
            by_h[at, :] = dy_ref[at, :] + (da * scale - wide * along).astype(jnp.bfloat16)

        tiles(tokens, tile, end)


def backward(h, dy, number, both, down, tile=512):
    tokens, d = h.shape
    steps = both.shape[2] // d
    whole = pl.BlockSpec((tokens, d), lambda q: (0, 0))
    gate_at = pl.BlockSpec((None, d, d), lambda q: (2 * number, 0, q))
    up_at = pl.BlockSpec((None, d, d), lambda q: (2 * number + 1, 0, q))
    down_at = pl.BlockSpec((None, d, d), lambda q: (number, q, 0))
    like = lambda v, count: jax.ShapeDtypeStruct((count, *v.shape[1:]), v.dtype)
    state = lambda t: pltpu.VMEM((tokens, d), t)
    flat = lambda: pltpu.VMEM((d, tokens), jnp.bfloat16)
    return pl.pallas_call(
        functools.partial(backward_kernel, steps, tile),
        grid=(steps,),
        out_shape=(like(both, 2), like(down, 1), jax.ShapeDtypeStruct(h.shape, h.dtype)),
        in_specs=[whole, whole, gate_at, up_at, down_at],
        out_specs=(pl.BlockSpec((2, d, d), lambda q: (0, 0, q)), pl.BlockSpec((None, d, d), lambda q: (0, q, 0)), whole),
        scratch_shapes=[
            state(jnp.bfloat16), flat(), flat(), state(jnp.bfloat16), state(jnp.bfloat16), state(jnp.bfloat16),
            state(jnp.float32), state(jnp.float32),
        ],
        compiler_params=pltpu.CompilerParams(dimension_semantics=("arbitrary",), vmem_limit_bytes=60 * 2**20),
        cost_estimate=pl.CostEstimate(flops=54_000_000_000, bytes_accessed=30_000_000, transcendentals=5_000_000),
        name="layer_backward",
    )(h, dy, both, both, down)


def place(ny, nz):
    s = lax.axis_index("s")
    return s // (2 * nz), lax.rem(s // 2, nz), lax.rem(s, 2)


def greet(peers):
    barrier = pltpu.get_barrier_semaphore()
    for peer in peers:
        pl.semaphore_signal(barrier, inc=1, device_id=peer, device_id_type=pl.DeviceIdType.MESH)
    pl.semaphore_wait(barrier, len(peers))


def remote(src, dst, send, recv, peer):
    return pltpu.make_async_remote_copy(
        src_ref=src, dst_ref=dst, send_sem=send, recv_sem=recv, device_id=peer, device_id_type=pl.DeviceIdType.MESH
    )


def ring(axis, y, z, c, ny, nz):
    n, pos = (ny, y) if axis == "y" else (nz, z)

    def at(k):
        return {"s": ((k * nz + z) if axis == "y" else (y * nz + k)) * 2 + c}

    return n, pos, (at(lax.rem(pos + 1, n)), at(lax.rem(pos + n - 1, n)))


def tile_of(ref, kind, s, first=0, count=40):
    if kind:
        return ref.at[:, pl.ds(pl.multiple_of(s * 40 + first, 8), count), :]
    width = ref.shape[2] // 4
    row, column = pl.multiple_of((s // 4) * 40 + first, 8), pl.multiple_of(lax.rem(s, 4) * width, 128)
    return ref.at[:, pl.ds(row, count), pl.ds(column, width)]


def loop(count, body):
    def run(i, _):
        body(i)
        return 0

    lax.fori_loop(0, count, run, 0)


PARTS = ((0, EDGE), (EDGE, 40 - EDGE))
WHOLE = (0, 40)


def gather_kernel(ny, nz, both_ref, down_ref, both_out, down_out, own_sem, pair_send, pair_recv, send1, recv1, send2, recv2):
    blocks, outs = (both_ref, down_ref), (both_out, down_out)
    y, z, c = place(ny, nz)
    me = (y * nz + z) * 2 + c
    partner = {"s": (y * nz + z) * 2 + (1 - c)}
    greet([partner, *ring("y", y, z, c, ny, nz)[2], *ring("z", y, z, c, ny, nz)[2]])
    own = [pltpu.make_async_copy(blocks[i], tile_of(outs[i], i, me), own_sem.at[i]) for i in range(2)]
    for copy in own:
        copy.start()
    for copy in own:
        copy.wait()

    def handed(yy, zz, core):
        at = yy * nz + zz
        refs = [tile_of(outs[i], i, at * 2 + core) for i in range(2)]
        return [remote(refs[i], refs[i], pair_send.at[at, i], pair_recv.at[at, i], partner) for i in range(2)]

    def hand(yy, zz):
        for copy in handed(yy, zz, c):
            copy.start()

    hand(y, z)

    def phase(axis, where, subs, send, recv):
        n, pos, to = ring(axis, y, z, c, ny, nz)
        h = n // 2

        def copies(d, t, j, ago):
            origin = lax.rem(pos + n - ago, n) if d == 0 else lax.rem(pos + ago, n)
            yy, zz = where(origin, j)
            first, rows = PARTS[d] if t == h - 1 else WHOLE
            refs = [tile_of(outs[i], i, (yy * nz + zz) * 2 + c, first, rows) for i in range(2)]
            return [remote(refs[i], refs[i], send.at[d, t, j, i], recv.at[d, t, j, i], to[d]) for i in range(2)], yy, zz

        for t in range(h):
            def advance(j, t=t):
                for d in (0, 1):
                    if t:
                        came, yy, zz = copies(d, t - 1, j, t)
                        for copy in came:
                            copy.wait_recv()
                    for copy in copies(d, t, j, t)[0]:
                        copy.start()
                    if t:
                        hand(yy, zz)

            loop(subs, advance)

        def last(j):
            for d in (0, 1):
                came, yy, zz = copies(d, h - 1, j, h)
                for copy in came:
                    copy.wait_recv()
            hand(yy, zz)

        loop(subs, last)

        def settle():
            def one(j):
                for t in range(h):
                    for d in (0, 1):
                        for copy in copies(d, t, j, t)[0]:
                            copy.wait_send()

            loop(subs, one)

        return settle

    @pl.when(c == 0)
    def _():
        settle1 = phase("y", lambda k, j: (k, z), 1, send1, recv1)
        settle2 = phase("z", lambda k, j: (j, k), ny, send2, recv2)
        settle1()
        settle2()

    @pl.when(c == 1)
    def _():
        settle1 = phase("z", lambda k, j: (y, k), 1, send1, recv1)
        settle2 = phase("y", lambda k, j: (k, j), nz, send2, recv2)
        settle1()
        settle2()

    def settle(i):
        for copy in handed(i // nz, lax.rem(i, nz), c):
            copy.wait_send()
        for copy in handed(i // nz, lax.rem(i, nz), 1 - c):
            copy.wait_recv()

    loop(ny * nz, settle)


def gathered(both, down, ny=NY, nz=NZ):
    dma = pltpu.SemaphoreType.DMA
    wide, tall = ((both.shape[0], ny * nz * 20, 4 * both.shape[2]), (down.shape[0], ny * nz * 80, down.shape[2]))
    return pl.pallas_call(
        functools.partial(gather_kernel, ny, nz),
        out_shape=[jax.ShapeDtypeStruct(shape, both.dtype) for shape in (wide, tall)],
        in_specs=[pl.BlockSpec(memory_space=pltpu.VMEM)] * 2,
        out_specs=[pl.BlockSpec(memory_space=pl.ANY)] * 2,
        scratch_shapes=[
            dma((2,)), dma((ny * nz, 2)), dma((ny * nz, 2)),
            dma((2, 4, 1, 2)), dma((2, 4, 1, 2)), dma((2, 4, 8, 2)), dma((2, 4, 8, 2)),
        ],
        compiler_params=pltpu.CompilerParams(collective_id=1, has_side_effects=True, vmem_limit_bytes=60 * 2**20),
        cost_estimate=pl.CostEstimate(flops=20_000_000_000, bytes_accessed=10_000_000, transcendentals=0),
        name="gather_plane",
    )(both, down)


def add(into, block, first=0, count=40):
    def one(i):
        at = pl.ds(first, count)
        into[i, at, :] = (into[i, at, :].astype(jnp.float32) + block[i, at, :].astype(jnp.float32)).astype(into.dtype)

    loop(3, one)


def over_planes(out, copies, nx):
    def one(i):
        total = copies[0, i].astype(jnp.float32)
        for k in range(1, nx):
            total += copies[k, i].astype(jnp.float32)
        out[i] = total.astype(out.dtype)

    loop(3, one)


def spread(source, copies, send, recv, nx):
    x = lax.axis_index("r")
    return [remote(source, copies.at[x], send.at[k - 1], recv.at[k - 1], {"r": lax.rem(x + k, nx)}) for k in range(1, nx)]


def keep(source, copies):
    x = lax.axis_index("r")

    def one(i):
        copies[x, i] = source[i]

    loop(3, one)


def reduce_kernel(nx, ny, nz, both_ref, down_ref, out_ref, mine, theirs, arrivals1, arrivals2, copies, own_sem,
                  pair_send, pair_recv, send1, recv1, send2, recv2, xsend, xrecv):
    grads, parts = (both_ref, down_ref), (pl.ds(0, 2), pl.ds(2, 1))
    x = lax.axis_index("r")
    y, z, c = place(ny, nz)
    partner = {"s": (y * nz + z) * 2 + (1 - c)}
    planes = [{"r": lax.rem(x + k, nx)} for k in range(1, nx)]
    greet([partner, *ring("y", y, z, c, ny, nz)[2], *ring("z", y, z, c, ny, nz)[2], *planes])

    def own(yy, zz):
        at = yy * nz + zz
        return [
            pltpu.make_async_copy(tile_of(grads[i], i, at * 2 + c), mine.at[yy, zz, parts[i]], own_sem.at[at, i])
            for i in range(2)
        ]

    def pair(yy, zz, core):
        at = yy * nz + zz
        return [
            remote(
                tile_of(grads[i], i, at * 2 + core), theirs.at[yy, zz, parts[i]], pair_send.at[at, i], pair_recv.at[at, i], partner
            )
            for i in range(2)
        ]

    def needed(n, pos):
        h = n // 2
        offsets = [h]
        for t in range(1, h):
            offsets += [h - t, n - h + t]
        return [lax.rem(pos + k, n) for k in [*offsets, 0]]

    def begin(copies):
        for copy in copies:
            copy.start()

    @pl.when(c == 0)
    def _():
        for k in needed(ny, y):
            loop(nz, lambda j, k=k: begin(pair(k, j, 1)))
        for k in needed(nz, z):
            loop(ny, lambda j, k=k: begin(own(j, k)))

    @pl.when(c == 1)
    def _():
        for k in needed(nz, z):
            loop(ny, lambda j, k=k: begin(pair(j, k, 0)))
        for k in needed(ny, y):
            loop(nz, lambda j, k=k: begin(own(k, j)))

    def both(yy, zz):
        for copy in own(yy, zz):
            copy.wait()
        for copy in pair(yy, zz, 1 - c):
            copy.wait_recv()
        add(mine.at[yy, zz], theirs.at[yy, zz])

    def phase(axis, block, subs, ready, arrivals, send, recv):
        n, pos, to = ring(axis, y, z, c, ny, nz)
        h = n // 2

        def rows_of(ref, d, t):
            return ref.at[:, pl.ds(*PARTS[d])] if t == 0 else ref

        def place_of(d, t):
            return lax.rem(pos + h - t, n) if d == 0 else lax.rem(pos + n - h + t, n)

        def out(d, t, j):
            return remote(
                rows_of(block(place_of(d, t), j), d, t), rows_of(arrivals.at[d, t * subs + j], d, t),
                send.at[d, t, j], recv.at[d, t, j], to[d],
            )

        def arrived(d, t, j, into):
            landed = arrivals.at[d, t * subs + j]
            part = rows_of(landed, d, t)
            remote(part, part, send.at[d, t, j], recv.at[d, t, j], to[d]).wait_recv()
            add(into, landed, *(PARTS[d] if t == 0 else WHOLE))

        for t in range(h):
            def advance(j, t=t):
                for d in (0, 1):
                    if t or d == 0:
                        ready(place_of(d, t), j)
                    if t:
                        arrived(d, t - 1, j, block(place_of(d, t), j))
                    out(d, t, j).start()

            loop(subs, advance)

        def last(j):
            ready(pos, j)
            for d in (0, 1):
                arrived(d, h - 1, j, block(pos, j))

        loop(subs, last)

        def settle():
            def one(j):
                for t in range(h):
                    for d in (0, 1):
                        out(d, t, j).wait_send()

            loop(subs, one)

        return settle

    def done(k, j):
        pass

    @pl.when(c == 0)
    def _():
        settle1 = phase("z", lambda k, j: mine.at[j, k], ny, lambda k, j: both(j, k), arrivals1, send1, recv1)
        settle2 = phase("y", lambda k, j: mine.at[k, z], 1, done, arrivals2, send2, recv2)
        settle1()
        settle2()

    @pl.when(c == 1)
    def _():
        settle1 = phase("y", lambda k, j: mine.at[k, j], nz, lambda k, j: both(k, j), arrivals1, send1, recv1)
        settle2 = phase("z", lambda k, j: mine.at[y, k], 1, done, arrivals2, send2, recv2)
        settle1()
        settle2()

    last = spread(mine.at[y, z], copies, xsend, xrecv, nx)
    for copy in last:
        copy.start()
    keep(mine.at[y, z], copies)
    for copy in last:
        copy.wait()
    over_planes(out_ref, copies, nx)

    def settle(i):
        for copy in pair(i // nz, lax.rem(i, nz), 1 - c):
            copy.wait_send()

    loop(ny * nz, settle)


def reduced(both, down, nx, ny=NY, nz=NZ):
    width = down.shape[2]
    dma = pltpu.SemaphoreType.DMA
    vmem = lambda *lead: pltpu.VMEM((*lead, 3, 40, width), jnp.bfloat16)
    return pl.pallas_call(
        functools.partial(reduce_kernel, nx, ny, nz),
        out_shape=jax.ShapeDtypeStruct((3, 40, width), jnp.bfloat16),
        in_specs=[pl.BlockSpec(memory_space=pl.ANY)] * 2,
        out_specs=pl.BlockSpec(memory_space=pltpu.VMEM),
        scratch_shapes=[
            vmem(ny, nz), vmem(ny, nz), vmem(2, ny * nz // 2), vmem(2, max(ny, nz) // 2), vmem(nx),
            dma((ny * nz, 2)), dma((ny * nz, 2)), dma((ny * nz, 2)),
            dma((2, 4, 8)), dma((2, 4, 8)), dma((2, 4, 1)), dma((2, 4, 1)), dma((max(nx - 1, 1),)), dma((max(nx - 1, 1),)),
        ],
        compiler_params=pltpu.CompilerParams(collective_id=2, has_side_effects=True, vmem_limit_bytes=60 * 2**20),
        cost_estimate=pl.CostEstimate(flops=40_000_000_000, bytes_accessed=20_000_000, transcendentals=0),
        name="reduce_all",
    )(both, down)


def planes_kernel(nx, b_ref, out_ref, copies, send, recv):
    x = lax.axis_index("r")
    greet([{"r": lax.rem(x + k, nx)} for k in range(1, nx)])
    sent = spread(b_ref, copies, send, recv, nx)
    for copy in sent:
        copy.start()
    keep(b_ref, copies)
    for copy in sent:
        copy.wait()
    over_planes(out_ref, copies, nx)


def across_planes(block, nx):
    dma = pltpu.SemaphoreType.DMA((nx - 1,))
    return pl.pallas_call(
        functools.partial(planes_kernel, nx),
        out_shape=jax.ShapeDtypeStruct(block.shape, block.dtype),
        in_specs=[pl.BlockSpec(memory_space=pltpu.VMEM)],
        out_specs=pl.BlockSpec(memory_space=pltpu.VMEM),
        scratch_shapes=[pltpu.VMEM((nx, *block.shape), block.dtype), dma, dma],
        compiler_params=pltpu.CompilerParams(collective_id=3, has_side_effects=True),
        cost_estimate=pl.CostEstimate(flops=5_000_000_000, bytes_accessed=1_000_000, transcendentals=0),
        name="across_planes",
    )(block)


def solution(mesh):
    nx = mesh.shape["r"]
    shards = mesh.shape["s"]
    fours = [[4 * g + m for m in range(4)] for g in range(shards // 4)]

    def step(x, dy, w_gate, w_up, w_down):
        rows = jnp.stack([w_gate, w_up], 1).reshape(2, 2, 10, 4, 640)
        rows = lax.all_to_all(rows, "s", 3, 2, axis_index_groups=fours, tiled=True).reshape(2, 2, 40, 640)
        both, down = gathered(rows.reshape(4, 40, 640), w_down)
        h0 = x[0]
        h1 = forward(h0, 0, both, down)
        by_both, by_down, by_h = backward(h1, dy[0], 1, both, down)
        parts = by_both.reshape(2, shards // 4, 40, 4, 640).transpose(1, 3, 0, 2, 4).reshape(shards, 80, 640)
        terms = jnp.concatenate([parts, by_down.reshape(shards, 40, 640)], 1).reshape(-1, 640)
        second = lax.psum_scatter(terms, "s", scatter_dimension=0, tiled=True).reshape(3, 40, 640)
        by_both, by_down, by_x = backward(h0, by_h, 0, both, down)
        one = reduced(by_both, by_down, nx)
        second, one = lax.optimization_barrier((second, one))
        both = jnp.stack([one, across_planes(second, nx)])
        rows = both[:, :2].reshape(2, 2, 40, 1, 640)
        rows = lax.all_to_all(rows, "s", 2, 3, axis_index_groups=fours, tiled=True).reshape(2, 2, 10, 2560)
        return by_x[None], rows[:, 0], rows[:, 1], both[:, 2]

    states, cut = P(("rep", "r", "s"), None, None), P(None, "s", None)
    return jax.shard_map(
        step,
        mesh=mesh,
        in_specs=(states, states) + (cut,) * 3,
        out_specs=(states,) + (P("rep", "s", None),) * 3,
        check_vma=False,
    )
```

time: 1210 us -> 429 us (0.35); the launches traced: 1200 us -> 429 us
  waiting for transfers between devices: 861 us -> 2.53 us
  Pallas kernels: 0 us -> 360 us
  matrix products: 281 us -> 0 us
    unnamed x13 -> x2, waiting for transfers between devices: 425 us -> 0.04 us
    all_gather x6 -> x0, waiting for transfers between devices: 394 us -> none  [fetched(): lax.all_gather(w[number], 's', axis=0, tiled=True)]
    pallas_call x0 -> x6, Pallas kernels: none -> 360 us  [the longest x2 176 us: backward(): pl.pallas_call(functools.partial(backward_kernel, steps, tile), grid=(ste...]
    dot_general x17 -> x0, matrix products: 281 us -> none  [the longest x6 110 us: layer(): up = jnp.dot(a, w['w_up'], preferred_element_type=jnp.float32)]
    psum x1 -> x0, waiting for transfers between devices: 42.6 us -> none  [summed(): lax.psum(lax.psum_scatter(term, 's', scatter_dimension=0, tiled=True), 'r')]
    reshape x0 -> x4, local copies, waits for them, and re-layouts: none -> 17.2 us  [the longest x2 16.2 us: step(): by_both.reshape(2, shards // 4, 40, 4, 640).transpose(1, 3, 0, 2, 4)]
    unnamed x36 -> x8, local copies, waits for them, and re-layouts: 15.5 us -> 1.5 us
  transfers between devices with their start and end apart: 10 -> 2, of which waited for: 10 -> 1; matrix products, arithmetic and copies ran while one was open for 14% -> 0% of each run, Pallas kernels for 0% -> 35%
where the time goes in v2:
time: 429 us
  Pallas kernels  360 us (84%)
  local copies, waits for them, and re-layouts  23.1 us (5%)
  between operations  14.2 us (3%)
  starting transfers between devices  10.3 us (2%)
  blocking collectives  10.1 us (2%)
  other arithmetic  7.94 us (2%)
    pallas_call x2, Pallas kernels, backward(): pl.pallas_call(functools.partial(backward_kernel, steps, tile), grid=(ste...  176 us
    pallas_call x1, Pallas kernels, gathered(): pl.pallas_call(functools.partial(gather_kernel, ny, nz), out_shape=[jax.S...  80.4 us
    pallas_call x1, Pallas kernels, reduced(): pl.pallas_call(functools.partial(reduce_kernel, nx, ny, nz), out_shape=ja...  60.5 us
    pallas_call x1, Pallas kernels, forward(): pl.pallas_call(functools.partial(forward_kernel, steps, tile), grid=(step...  33.9 us
    reshape x2, local copies, waits for them, and re-layouts, step(): by_both.reshape(2, shards // 4, 40, 4, 640).transpose(1, 3, 0, 2, 4)  16.2 us
    all_to_all x1, starting transfers between devices, step(): lax.all_to_all(rows, 's', 2, 3, axis_index_groups=fours, tiled=True)  10.3 us
    all_to_all x1, blocking collectives, step(): lax.all_to_all(rows, 's', 3, 2, axis_index_groups=fours, tiled=True)  10.1 us
    pallas_call x1, Pallas kernels, across_planes(): pl.pallas_call(functools.partial(planes_kernel, nx), out_shape=jax.ShapeD...  9.07 us
  transfers between devices with their start and end apart: 2, of which 1 were waited for; matrix products, arithmetic and copies ran while one was open for 0% of the time, Pallas kernels for 35%

profile of v2, /device:TPU:1, one launch (start us, length us, event | category | flops | bytes accessed | tf_op | source)
XLA Modules:
  0.0 428.5 jit_solution(7666147968934773257)
XLA Ops:
  7.2 0.0 reduce-scatter.4.cloned.1.call-start
  7.2 1.0 stack.18
  8.2 0.2 copy.33
  8.3 1.0 stack.19
  9.3 0.2 copy.34
  9.5 0.5 pad_maximum_fusion.1
  10.0 10.1 %all_to_all.30 = bf16[2,2,10,4,640]{4,1,0,2,3:T(2,128)(2,1)S(1)} all-to-all(bf16[2,2,10,4,640]{4,1,0,2,3:T(2,128)(2,1)S(1)} %pad_maximum_fusion.1), channel_id=1, replica_groups={{0,1,2,3},{4,5,6,7},{8,9,10,11},{12,13,14,15},{16,17,18,19},{20,21,22,2..., dimensions={3} | all-to-all | bytes 409600 | tf_op jit(solution)/shard_map/all_to_all | solution.py:539
  20.1 0.1 reshape_reshape.3
  20.2 0.7 copy.35.both_ref
  20.9 0.0 copy-start
  20.9 80.4 %gather_plane.1 = (bf16[4,640,2560]{2,1,0:T(8,128)(2,1)}, bf16[2,2560,640]{2,1,0:T(8,128)(2,1)}) custom-call(bf16[4,40,640]{2,1,0:T(8,128)(2,1)} %copy.35.both_ref, bf16[2,40,640]{2,1,0:T(8,128)(2,1)} %down_ref.1), custom_call_target="tpu_custom_call" | custom-call | flops 20000000000 | bytes 10000000 | tf_op jit(solution)/shard_map/gather_plane/pallas_call | solution.py:300
  101.3 0.0 copy-done
  101.4 33.9 %layer_forward.1.h_ref = bf16[2048,640]{1,0:T(8,128)(2,1)S(1)} custom-call(bf16[2048,640]{1,0:T(8,128)(2,1)S(1)} %bitcast.35, bf16[4,640,2560]{2,1,0:T(8,128)(2,1)} %get-tuple-element.14.g_ref.u_ref, bf16[4,640,2560]{2,1,0:T(8,128)(2,1)} %get-tuple-element.14.g_ref.u_ref, bf16[2,2560,640]{2,1,0:T(8,128)(2,1)} %get-tuple-element.15.d_ref), custom_call_target="tpu_custom_call" | custom-call | flops 20000000000 | bytes 15000000 | tf_op jit(solution)/shard_map/layer_forward/pallas_call | solution.py:70
  135.3 0.0 copy-start.1
  135.3 1.5 copy-done.1
  136.8 88.3 %layer_backward.2 = (bf16[2,640,2560]{2,1,0:T(8,128)(2,1)}, bf16[1,2560,640]{2,1,0:T(8,128)(2,1)}, bf16[2048,640]{1,0:T(8,128)(2,1)}) custom-call(bf16[2048,640]{1,0:T(8,128)(2,1)} %copy-done.1, bf16[2048,640]{1,0:T(8,128)(2,1)} %bitcast.45, bf16[4,640,2560]{2,1,0:T(8,128)(2,1)} %get-tuple-element.14.g_ref.u_ref, ...), custom_call_target="tpu_custom_call" | custom-call | flops 54000001024 | bytes 30000000 | tf_op jit(solution)/shard_map/layer_backward/pallas_call | solution.py:143
  225.1 12.2 %reshape.36 = bf16[2,16,40,4,640]{4,3,2,1,0:T(4,128)(2,1)} reshape(bf16[2,640,2560]{2,1,0:T(8,128)(2,1)} %get-tuple-element.18) | data formatting | bytes 13107200 | tf_op jit(solution)/shard_map/reshape | solution.py:544
  237.2 0.0 copy-start.2
  237.2 4.1 copy.36
  241.3 0.0 copy-done.2
  241.3 5.1 %pad_maximum_fusion = bf16[64,120,640]{2,1,0:T(8,128)(2,1)} fusion(bf16[64,40,640]{2,1,0:T(8,128)(2,1)S(1)} %bitcast.38, bf16[64,80,640]{2,1,0:T(8,128)(2,1)S(1)} %bitcast.37), kind=kLoop, calls=%fused_computation | loop fusion | flops 19660800 | bytes 19660800 | tf_op jit(solution)/shard_map/concatenate | solution.py:545
  246.4 0.0 reduce-scatter.4.cloned.1.call-update
  246.4 88.1 %layer_backward.3 = (bf16[2,640,2560]{2,1,0:T(8,128)(2,1)}, bf16[1,2560,640]{2,1,0:T(8,128)(2,1)}, bf16[2048,640]{1,0:T(8,128)(2,1)}) custom-call(bf16[2048,640]{1,0:T(8,128)(2,1)} %bitcast.34, bf16[2048,640]{1,0:T(8,128)(2,1)} %get-tuple-element.16.dy_ref, bf16[4,640,2560]{2,1,0:T(8,128)(2,1)} %get-tuple-element.14.g_ref.u_ref, ...), custom_call_target="tpu_custom_call" | custom-call | flops 54000001024 | bytes 30000000 | tf_op jit(solution)/shard_map/layer_backward/pallas_call | solution.py:143
  334.5 60.5 %reduce_all.1 = bf16[3,40,640]{2,1,0:T(8,128)(2,1)} custom-call(bf16[2,640,2560]{2,1,0:T(8,128)(2,1)} %get-tuple-element.20.both_ref, bf16[1,2560,640]{2,1,0:T(8,128)(2,1)} %get-tuple-element.21.down_ref), custom_call_target="tpu_custom_call" | custom-call | flops 40000000000 | bytes 20000000 | tf_op jit(solution)/shard_map/reduce_all/pallas_call | solution.py:490
  395.1 0.0 reduce-scatter.4.cloned.1.call-done
  395.1 0.0 copy-start.3
  395.1 9.1 %across_planes.1 = bf16[3,40,640]{2,1,0:T(8,128)(2,1)} custom-call(bf16[3,40,640]{2,1,0:T(8,128)(2,1)} %bitcast.46), custom_call_target="tpu_custom_call" | custom-call | flops 5000000000 | bytes 1000000 | tf_op jit(solution)/shard_map/across_planes/pallas_call | solution.py:520
  404.2 0.0 copy-done.3
  404.2 0.9 fusion.1
  405.1 0.8 copy.37
  406.0 10.3 %all-to-all-start.1 = ((bf16[2,2,40,1,640]{4,1,0,3,2:T(2,128)(2,1)}), bf16[2,2,40,1,640]{4,1,0,3,2:T(2,128)(2,1)S(1)}, u32[]{:S(2)}, u32[]{:S(2)}) async-start(bf16[2,2,40,1,640]{4,1,0,3,2:T(2,128)(2,1)} %copy.37), calls=%async_computation.1 | async-start | bytes 409600 | tf_op jit(solution)/shard_map/all_to_all | solution.py:552
  416.2 1.5 fusion.2
  417.7 2.5 all-to-all-done.1
  420.2 0.1 copy.38
  420.3 0.1 copy.39
  420.4 0.1 reshape.42
  420.5 0.3 fusion.3
  420.8 0.9 copy_bitcast_fusion
Async XLA Ops:
  7.2 387.9 %reduce-scatter.4.cloned.1.call-start = ((), (), s32[]{:S(2)}) async-start(), calls=%async_computation.3 | async-start | bytes 9984000
  20.9 80.5 %copy-start = (bf16[1,2048,640]{2,1,0:T(8,128)(2,1)S(1)}, bf16[1,2048,640]{2,1,0:T(8,128)(2,1)}, u32[]{:S(2)}) copy-start(bf16[1,2048,640]{2,1,0:T(8,128)(2,1)} %param.5) | copy-start | bytes 7864324
  135.3 1.5 copy-start.1
  237.2 4.1 copy-start.2
  395.1 9.1 %copy-start.3 = (bf16[3,40,640]{2,1,0:T(8,128)(2,1)S(1)}, bf16[3,40,640]{2,1,0:T(8,128)(2,1)}, u32[]{:S(2)}) copy-start(bf16[3,40,640]{2,1,0:T(8,128)(2,1)} %reduce_all.1) | copy-start | bytes 460804
  406.0 14.2 %all-to-all-start.1 = ((bf16[2,2,40,1,640]{4,1,0,3,2:T(2,128)(2,1)}), bf16[2,2,40,1,640]{4,1,0,3,2:T(2,128)(2,1)S(1)}, u32[]{:S(2)}, u32[]{:S(2)}) async-start(bf16[2,2,40,1,640]{4,1,0,3,2:T(2,128)(2,1)} %copy.37), calls=%async_computation.1 | async-start | bytes 409600 | tf_op jit(solution)/shard_map/all_to_all | solution.py:552
Sparse Core Ops, SparseCore 0:
  246.6 145.3 reduce-scatter.3

commit v3 on v2

--- a/solution.py
+++ b/solution.py
@@ -23,12 +23,12 @@
     return lax.dot_general(a, b, (((1,), (1,)), ((), ())), preferred_element_type=jnp.float32)
 
 
-def tiles(count, size, body):
+def tiles(count, size, body, unroll=False):
     def run(i, _):
         body(pl.ds(pl.multiple_of(i * size, size), size))
         return 0
 
-    lax.fori_loop(0, count // size, run, 0)
+    lax.fori_loop(0, count // size, run, 0, unroll=unroll)
 
 
 def forward_kernel(steps, tile, h_ref, g_ref, u_ref, d_ref, y_ref, a_ref, total):
@@ -40,9 +40,9 @@
         def start(at):
             wide = h_ref[at, :].astype(jnp.float32)
             a_ref[at, :] = (wide * scale_of(wide)).astype(jnp.bfloat16)
-            total[at, :] = jnp.zeros((tile, h_ref.shape[1]), jnp.float32)
-
-        tiles(tokens, tile, start)
+            total[at, :] = jnp.zeros((256, h_ref.shape[1]), jnp.float32)
+
+        tiles(tokens, 256, start)
 
     def main(at):
         a = a_ref[at, :]
@@ -57,16 +57,16 @@
         def end(at):
             y_ref[at, :] = h_ref[at, :] + total[at, :].astype(jnp.bfloat16)
 
-        tiles(tokens, tile, end)
-
-
-def forward(h, number, both, down, tile=512):
+        tiles(tokens, 256, end)
+
+
+def forward(h, number, both, down, tile=1024, cut=512):
     tokens, d = h.shape
-    steps = both.shape[2] // d
-    whole = pl.BlockSpec((tokens, d), lambda q: (0, 0))
-    gate_at = pl.BlockSpec((None, d, d), lambda q: (2 * number, 0, q))
-    up_at = pl.BlockSpec((None, d, d), lambda q: (2 * number + 1, 0, q))
-    down_at = pl.BlockSpec((None, d, d), lambda q: (number, q, 0))
+    steps = both.shape[2] // cut
+    whole = pl.BlockSpec((tokens, d), lambda q: (0, 0), pipeline_mode=pl.Buffered(1))
+    gate_at = pl.BlockSpec((None, d, cut), lambda q: (2 * number, 0, q))
+    up_at = pl.BlockSpec((None, d, cut), lambda q: (2 * number + 1, 0, q))
+    down_at = pl.BlockSpec((None, cut, d), lambda q: (number, q, 0))
     return pl.pallas_call(
         functools.partial(forward_kernel, steps, tile),
         grid=(steps,),
@@ -93,10 +93,10 @@
             a_ref[at, :] = a
             at_ref[:, at] = a.T
             dyt_ref[:, at] = dy_ref[at, :].T
-            total_g[at, :] = jnp.zeros((tile, d), jnp.float32)
-            total_u[at, :] = jnp.zeros((tile, d), jnp.float32)
-
-        tiles(tokens, tile, start)
+            total_g[at, :] = jnp.zeros((256, d), jnp.float32)
+            total_u[at, :] = jnp.zeros((256, d), jnp.float32)
+
+        tiles(tokens, 256, start)
 
     def main(at):
         a = a_ref[at, :]
@@ -127,27 +127,28 @@
             along = jnp.sum(da * wide, -1, keepdims=True) * (scale * scale * scale) * (1.0 / d)
             by_h[at, :] = dy_ref[at, :] + (da * scale - wide * along).astype(jnp.bfloat16)
 
-        tiles(tokens, tile, end)
-
-
-def backward(h, dy, number, both, down, tile=512):
+        tiles(tokens, 256, end)
+
+
+def backward(h, dy, number, both, down, tile=1024, cut=512):
     tokens, d = h.shape
-    steps = both.shape[2] // d
-    whole = pl.BlockSpec((tokens, d), lambda q: (0, 0))
-    gate_at = pl.BlockSpec((None, d, d), lambda q: (2 * number, 0, q))
-    up_at = pl.BlockSpec((None, d, d), lambda q: (2 * number + 1, 0, q))
-    down_at = pl.BlockSpec((None, d, d), lambda q: (number, q, 0))
+    steps = both.shape[2] // cut
+    whole = pl.BlockSpec((tokens, d), lambda q: (0, 0), pipeline_mode=pl.Buffered(1))
+    gate_at = pl.BlockSpec((None, d, cut), lambda q: (2 * number, 0, q))
+    up_at = pl.BlockSpec((None, d, cut), lambda q: (2 * number + 1, 0, q))
+    down_at = pl.BlockSpec((None, cut, d), lambda q: (number, q, 0))
     like = lambda v, count: jax.ShapeDtypeStruct((count, *v.shape[1:]), v.dtype)
     state = lambda t: pltpu.VMEM((tokens, d), t)
+    hidden = lambda: pltpu.VMEM((tokens, cut), jnp.bfloat16)
     flat = lambda: pltpu.VMEM((d, tokens), jnp.bfloat16)
     return pl.pallas_call(
         functools.partial(backward_kernel, steps, tile),
         grid=(steps,),
         out_shape=(like(both, 2), like(down, 1), jax.ShapeDtypeStruct(h.shape, h.dtype)),
         in_specs=[whole, whole, gate_at, up_at, down_at],
-        out_specs=(pl.BlockSpec((2, d, d), lambda q: (0, 0, q)), pl.BlockSpec((None, d, d), lambda q: (0, q, 0)), whole),
+        out_specs=(pl.BlockSpec((2, d, cut), lambda q: (0, 0, q)), pl.BlockSpec((None, cut, d), lambda q: (0, q, 0)), whole),
         scratch_shapes=[
-            state(jnp.bfloat16), flat(), flat(), state(jnp.bfloat16), state(jnp.bfloat16), state(jnp.bfloat16),
+            state(jnp.bfloat16), flat(), flat(), hidden(), hidden(), hidden(),
             state(jnp.float32), state(jnp.float32),
         ],
         compiler_params=pltpu.CompilerParams(dimension_semantics=("arbitrary",), vmem_limit_bytes=60 * 2**20),
@@ -537,12 +538,17 @@
     def step(x, dy, w_gate, w_up, w_down):
         rows = jnp.stack([w_gate, w_up], 1).reshape(2, 2, 10, 4, 640)
         rows = lax.all_to_all(rows, "s", 3, 2, axis_index_groups=fours, tiled=True).reshape(2, 2, 40, 640)
-        both, down = gathered(rows.reshape(4, 40, 640), w_down)
+        blocks = lax.all_gather(jnp.concatenate([rows[1].reshape(80, 640), w_down[1]]), "s", axis=0, tiled=True)
+        blocks = blocks.reshape(shards // 4, 4, 3, 40, 640)
+        both, down = gathered(rows[0], w_down[:1])
         h0 = x[0]
         h1 = forward(h0, 0, both, down)
-        by_both, by_down, by_h = backward(h1, dy[0], 1, both, down)
-        parts = by_both.reshape(2, shards // 4, 40, 4, 640).transpose(1, 3, 0, 2, 4).reshape(shards, 80, 640)
-        terms = jnp.concatenate([parts, by_down.reshape(shards, 40, 640)], 1).reshape(-1, 640)
+        next_both = jnp.concatenate([blocks[:, m, :2].swapaxes(0, 1).reshape(2, 640, 640) for m in range(4)], 2)
+        next_down = blocks[:, :, 2].reshape(1, 2560, 640)
+        by_both, by_down, by_h = backward(h1, dy[0], 0, next_both, next_down)
+        parts = [by_both[:, :, 640 * m : 640 * m + 640].reshape(2, shards // 4, 40, 640) for m in range(4)]
+        parts = jnp.stack([part[i] for part in parts for i in range(2)], 1).reshape(shards, 2, 40, 640)
+        terms = jnp.concatenate([parts, by_down.reshape(shards, 1, 40, 640)], 1).reshape(-1, 640)
         second = lax.psum_scatter(terms, "s", scatter_dimension=0, tiled=True).reshape(3, 40, 640)
         by_both, by_down, by_x = backward(h0, by_h, 0, both, down)
         one = reduced(by_both, by_down, nx)

time: 429 us -> 398 us (0.928)
  Pallas kernels: 360 us -> 317 us
  blocking collectives: 10.1 us -> 0 us
  other arithmetic: 7.94 us -> 14.1 us
  starting transfers between devices: 10.3 us -> 16.1 us
  waiting for transfers between devices: 2.53 us -> 7.95 us
  local copies, waits for them, and re-layouts: 23.1 us -> 28.5 us
    pallas_call x1, Pallas kernels: 80.4 us -> 53.1 us  [gathered(): pl.pallas_call(functools.partial(gather_kernel, ny, nz), out_shape=[jax.S...]
    pallas_call x2, Pallas kernels: 176 us -> 159 us  [backward(): pl.pallas_call(functools.partial(backward_kernel, steps, tile), grid=(ste...]
    reshape x2 -> x0, local copies, waits for them, and re-layouts: 16.2 us -> none  [step(): by_both.reshape(2, shards // 4, 40, 4, 640).transpose(1, 3, 0, 2, 4)]
    all_to_all x1 -> x0, blocking collectives: 10.1 us -> none  [step(): lax.all_to_all(rows, 's', 3, 2, axis_index_groups=fours, tiled=True)]
    slice x0 -> x4, local copies, waits for them, and re-layouts: none -> 7.73 us  [the longest x1 3.93 us: step(): next_down = blocks[:, :, 2].reshape(1, 2560, 640)]
    unnamed x8 -> x15, local copies, waits for them, and re-layouts: 1.5 us -> 8.48 us
    all_to_all x0 -> x1, starting transfers between devices: none -> 6.51 us  [step(): lax.all_to_all(rows, 's', 3, 2, axis_index_groups=fours, tiled=True)]
    concatenate x1 -> x3, other arithmetic: 5.09 us -> 11.6 us  [the longest x1 7.63 us: step(): jnp.concatenate([parts, by_down.reshape(shards, 1, 40, 640)], 1)]
  transfers between devices with their start and end apart: 2 -> 4, of which waited for: 1 -> 3; matrix products, arithmetic and copies ran while one was open for 0% -> 1% of each run, Pallas kernels for 35% -> 57%
where the time goes in v3:
time: 398 us
  Pallas kernels  317 us (80%)
  local copies, waits for them, and re-layouts  28.5 us (7%)
  starting transfers between devices  16.1 us (4%)
  between operations  14.2 us (4%)
  other arithmetic  14.1 us (4%)
  waiting for transfers between devices  7.95 us (2%)
    pallas_call x2, Pallas kernels, backward(): pl.pallas_call(functools.partial(backward_kernel, steps, tile), grid=(ste...  159 us
    pallas_call x1, Pallas kernels, reduced(): pl.pallas_call(functools.partial(reduce_kernel, nx, ny, nz), out_shape=ja...  66.1 us
    pallas_call x1, Pallas kernels, gathered(): pl.pallas_call(functools.partial(gather_kernel, ny, nz), out_shape=[jax.S...  53.1 us
    pallas_call x1, Pallas kernels, forward(): pl.pallas_call(functools.partial(forward_kernel, steps, tile), grid=(step...  29.6 us
    all_to_all x1, starting transfers between devices, step(): lax.all_to_all(rows, 's', 2, 3, axis_index_groups=fours, tiled=True)  9.51 us
    pallas_call x1, Pallas kernels, across_planes(): pl.pallas_call(functools.partial(planes_kernel, nx), out_shape=jax.ShapeD...  9.08 us
    unnamed x15, local copies, waits for them, and re-layouts  8.48 us
  transfers between devices with their start and end apart: 4, of which 3 were waited for; matrix products, arithmetic and copies ran while one was open for 1% of the time, Pallas kernels for 57%

profile of v3, /device:TPU:1, one launch (start us, length us, event | category | flops | bytes accessed | tf_op | source)
XLA Modules:
  0.0 397.7 jit_solution(15649178508065387206)
XLA Ops:
  7.2 1.0 stack.21
  8.1 1.0 stack.22
  9.1 0.1 pad_maximum_fusion.2
  9.2 0.8 copy.93
  10.1 6.5 %all-to-all-start = ((bf16[2,2,10,4,640]{4,1,2,0,3:T(2,128)(2,1)}), bf16[2,2,10,4,640]{4,1,2,0,3:T(2,128)(2,1)S(1)}, u32[]{:S(2)}, u32[]{:S(2)}) async-start(bf16[2,2,10,4,640]{4,1,2,0,3:T(2,128)(2,1)} %copy.93), calls=%async_computation | async-start | bytes 409600 | tf_op jit(solution)/shard_map/all_to_all | solution.py:540
  16.6 1.5 slice_bitcast_fusion.4
  18.1 2.5 all-to-all-done
  20.5 0.1 fusion.5
  20.8 0.7 pad_maximum_fusion.3
  21.5 0.0 all-gather.2.cloned.1.call-update
  21.5 0.0 reduce-scatter.4.cloned.1.call-start
  21.5 0.7 copy.94.both_ref
  22.2 53.1 %gather_plane.1 = (bf16[2,640,2560]{2,1,0:T(8,128)(2,1)}, bf16[1,2560,640]{2,1,0:T(8,128)(2,1)}) custom-call(bf16[2,40,640]{2,1,0:T(8,128)(2,1)} %copy.94.both_ref, bf16[1,40,640]{2,1,0:T(8,128)(2,1)} %get-tuple-element.45.down_ref), custom_call_target="tpu_custom_call" | custom-call | flops 20000000000 | bytes 10000000 | tf_op jit(solution)/shard_map/gather_plane/pallas_call | solution.py:301
  75.3 29.6 %layer_forward.1.h_ref = bf16[2048,640]{1,0:T(8,128)(2,1)S(1)} custom-call(bf16[2048,640]{1,0:T(8,128)(2,1)S(1)} %bitcast.84, bf16[2,640,2560]{2,1,0:T(8,128)(2,1)} %get-tuple-element.14.g_ref.u_ref, bf16[2,640,2560]{2,1,0:T(8,128)(2,1)} %get-tuple-element.14.g_ref.u_ref, bf16[1,2560,640]{2,1,0:T(8,128)(2,1)} %get-tuple-element.15.d_ref), custom_call_target="tpu_custom_call" | custom-call | flops 20000000000 | bytes 15000000 | tf_op jit(solution)/shard_map/layer_forward/pallas_call | solution.py:70
  105.0 1.5 copy-done.1
  106.5 2.9 all-gather.2.cloned.1.call-done
  109.4 3.9 slice.112
  113.3 3.5 slice_bitcast_fusion.3
  116.8 0.1 copy.96
  117.0 0.1 copy.99
  117.1 0.1 copy.98
  117.3 0.1 copy.97
  117.4 3.3 pad_maximum_fusion.1.g_ref.u_ref
  120.7 79.5 %layer_backward.2 = (bf16[2,640,2560]{2,1,0:T(8,128)(2,1)}, bf16[1,2560,640]{2,1,0:T(8,128)(2,1)}, bf16[2048,640]{1,0:T(8,128)(2,1)}) custom-call(bf16[2048,640]{1,0:T(8,128)(2,1)} %copy-done.1, bf16[2048,640]{1,0:T(8,128)(2,1)} %bitcast.109, bf16[2,640,2560]{2,1,0:T(8,128)(2,1)} %pad_maximum_fusion.1.g_ref.u_ref, ...), custom_call_target="tpu_custom_call" | custom-call | flops 54000001024 | bytes 30000000 | tf_op jit(solution)/shard_map/layer_backward/pallas_call | solution.py:144
  200.2 3.6 fusion.3
  203.8 1.0 constant_dynamic-update-slice_fusion.7
  204.8 1.0 constant_dynamic-update-slice_fusion.6
  205.8 1.0 constant_dynamic-update-slice_fusion.5
  206.8 1.0 constant_dynamic-update-slice_fusion.4
  207.8 1.0 constant_dynamic-update-slice_fusion.3
  208.7 1.0 constant_dynamic-update-slice_fusion.2
  209.7 1.1 constant_dynamic-update-slice_fusion.1
  210.8 1.0 constant_dynamic-update-slice_fusion
  211.8 7.6 %pad_maximum_fusion = bf16[64,3,40,640]{3,2,1,0:T(8,128)(2,1)} fusion(bf16[64,1,40,640]{3,2,1,0:T(8,128)(2,1)S(1)} %bitcast.92, bf16[64,2,40,640]{3,2,1,0:T(8,128)(2,1)} %bitcast.38), kind=kLoop, calls=%fused_computation | loop fusion | flops 4915200 | bytes 19660800 | tf_op jit(solution)/shard_map/concatenate | solution.py:551
  219.4 79.5 %layer_backward.3 = (bf16[2,640,2560]{2,1,0:T(8,128)(2,1)}, bf16[1,2560,640]{2,1,0:T(8,128)(2,1)}, bf16[2048,640]{1,0:T(8,128)(2,1)}) custom-call(bf16[2048,640]{1,0:T(8,128)(2,1)} %bitcast.83, bf16[2048,640]{1,0:T(8,128)(2,1)} %get-tuple-element.16.dy_ref, bf16[2,640,2560]{2,1,0:T(8,128)(2,1)} %get-tuple-element.14.g_ref.u_ref, ...), custom_call_target="tpu_custom_call" | custom-call | flops 54000001024 | bytes 30000000 | tf_op jit(solution)/shard_map/layer_backward/pallas_call | solution.py:144
  299.0 66.1 %reduce_all.1 = bf16[3,40,640]{2,1,0:T(8,128)(2,1)} custom-call(bf16[2,640,2560]{2,1,0:T(8,128)(2,1)} %get-tuple-element.20.both_ref, bf16[1,2560,640]{2,1,0:T(8,128)(2,1)} %get-tuple-element.21.down_ref), custom_call_target="tpu_custom_call" | custom-call | flops 40000000000 | bytes 20000000 | tf_op jit(solution)/shard_map/reduce_all/pallas_call | solution.py:491
  365.0 0.0 reduce-scatter.4.cloned.1.call-done
  365.1 9.1 %across_planes.1 = bf16[3,40,640]{2,1,0:T(8,128)(2,1)} custom-call(bf16[3,40,640]{2,1,0:T(8,128)(2,1)} %bitcast.110), custom_call_target="tpu_custom_call" | custom-call | flops 5000000000 | bytes 1000000 | tf_op jit(solution)/shard_map/across_planes/pallas_call | solution.py:521
  374.2 0.9 fusion.1
  375.1 0.8 copy.109
  375.9 9.5 %all-to-all-start.1 = ((bf16[2,2,40,1,640]{4,1,0,3,2:T(2,128)(2,1)}), bf16[2,2,40,1,640]{4,1,0,3,2:T(2,128)(2,1)S(1)}, u32[]{:S(2)}, u32[]{:S(2)}) async-start(bf16[2,2,40,1,640]{4,1,0,3,2:T(2,128)(2,1)} %copy.109), calls=%async_computation.1 | async-start | bytes 409600 | tf_op jit(solution)/shard_map/all_to_all | solution.py:558
  385.4 1.5 fusion.2
  386.9 2.5 all-to-all-done.1
  389.4 0.1 copy.110
  389.5 0.1 copy.111
  389.6 0.1 reshape.83
  389.7 0.3 fusion.4
  390.0 0.9 copy_bitcast_fusion
  (11 shorter events, 0.1 us)
Async XLA Ops:
  10.1 10.5 %all-to-all-start = ((bf16[2,2,10,4,640]{4,1,2,0,3:T(2,128)(2,1)}), bf16[2,2,10,4,640]{4,1,2,0,3:T(2,128)(2,1)S(1)}, u32[]{:S(2)}, u32[]{:S(2)}) async-start(bf16[2,2,10,4,640]{4,1,2,0,3:T(2,128)(2,1)} %copy.93), calls=%async_computation | async-start | bytes 409600 | tf_op jit(solution)/shard_map/all_to_all | solution.py:540
  16.6 92.8 %all-gather.2.cloned.1.call-start = ((), (), s32[]{:S(2)}) async-start(), calls=%async_computation.3 | async-start | bytes 9984000 | tf_op jit(solution)/shard_map/all_gather | solution.py:541
  21.5 343.6 %reduce-scatter.4.cloned.1.call-start = ((), (), s32[]{:S(2)}) async-start(), calls=%async_computation.4 | async-start | bytes 9984000
  22.2 53.1 %copy-start = (bf16[1,2048,640]{2,1,0:T(8,128)(2,1)S(1)}, bf16[1,2048,640]{2,1,0:T(8,128)(2,1)}, u32[]{:S(2)}) copy-start(bf16[1,2048,640]{2,1,0:T(8,128)(2,1)} %param.5) | copy-start | bytes 7864324
  105.0 1.5 copy-start.1
  203.8 8.0 %copy-start.2 = (bf16[1,2560,640]{2,1,0:T(8,128)(2,1)S(1)}, bf16[1,2560,640]{2,1,0:T(8,128)(2,1)}, u32[]{:S(2)}) copy-start(bf16[1,2560,640]{2,1,0:T(8,128)(2,1)} %get-tuple-element.19) | copy-start | bytes 9830404
  365.1 9.1 %copy-start.3 = (bf16[3,40,640]{2,1,0:T(8,128)(2,1)S(1)}, bf16[3,40,640]{2,1,0:T(8,128)(2,1)}, u32[]{:S(2)}) copy-start(bf16[3,40,640]{2,1,0:T(8,128)(2,1)} %reduce_all.1) | copy-start | bytes 460804
  375.9 13.5 %all-to-all-start.1 = ((bf16[2,2,40,1,640]{4,1,0,3,2:T(2,128)(2,1)}), bf16[2,2,40,1,640]{4,1,0,3,2:T(2,128)(2,1)S(1)}, u32[]{:S(2)}, u32[]{:S(2)}) async-start(bf16[2,2,40,1,640]{4,1,0,3,2:T(2,128)(2,1)} %copy.109), calls=%async_computation.1 | async-start | bytes 409600 | tf_op jit(solution)/shard_map/all_to_all | solution.py:558
Sparse Core Ops, SparseCore 0:
  21.6 87.7 all-gather.1
  219.6 145.1 reduce-scatter.3
